TPU v7x, 8 devices: a whole 2x2x1 slice. The times are simulated.
8 devices in a mesh: dp: 1 (over z), tp: 2 (over y), cp: 4 (over x, core).
Axes of the slice: x: 2, y: 2, z: 1, core: 2. Of those that a mesh axis runs over, the one named last changes fastest.
Arguments:
- x_tokens: bfloat16 [256, 3072], P(('dp', 'cp', 'tp'))
- w_q: bfloat16 [3072, 16, 256], P(None, 'tp')
- w_k: bfloat16 [3072, 16, 256], P(None, 'tp')
- w_v: bfloat16 [3072, 16, 256], P(None, 'tp')
- w_o: bfloat16 [16, 256, 3072], P('tp')
Outputs:
- output: bfloat16 [256, 3072], P(('dp', 'cp', 'tp'))
All inputs are finite; a program needn't handle non-finite values.
Results may differ from a plain program's by a relative error of at most 0.00540522.
Values are sent between devices in bfloat16 or wider.
A program may use at most 1 GiB of HBM per device.

v0:
```python
import jax
import jax.numpy as jnp
from jax import lax
from jax.sharding import PartitionSpec as P

NEG_BIG = -1e30


def online_update(q_blk, k_blk, v_blk, softmax_state, causal_mask):
    row_max, row_sum, out_acc = softmax_state
    inv_sqrt = q_blk.shape[-1] ** -0.5
    scores = jnp.einsum('qhe,khe->hqk', q_blk, k_blk, preferred_element_type=jnp.float32) * inv_sqrt
    if causal_mask is not None:
        scores = jnp.where(causal_mask, scores, NEG_BIG)
    new_max = jnp.maximum(row_max, scores.max(axis=-1))
    rescale = jnp.exp(row_max - new_max)
    weights = jnp.exp(scores - new_max[..., None])
    new_sum = rescale * row_sum + weights.sum(axis=-1)
    new_acc = rescale[..., None] * out_acc + jnp.einsum('hqk,khe->hqe', weights.astype(jnp.bfloat16), v_blk, preferred_element_type=jnp.float32)
    return new_max, new_sum, new_acc


def empty_state(n_heads, n_rows, head_dim):
    return (jnp.full((n_heads, n_rows), NEG_BIG, jnp.float32), jnp.zeros((n_heads, n_rows), jnp.float32), jnp.zeros((n_heads, n_rows, head_dim), jnp.float32))


def solution(mesh):
    cp_size = mesh.shape['cp']
    send_perm = [(rank_from, (rank_from + 1) % cp_size) for rank_from in range(cp_size)]

    def device_fn(x_loc, w_q, w_k, w_v, w_o):
        x_shard = lax.all_gather(x_loc, 'tp', axis=0, tiled=True)
        shard_len = x_shard.shape[0]
        block_len = shard_len // 2
        n_heads = w_q.shape[1]
        head_dim = w_q.shape[2]

        def project(weight):
            return jnp.einsum('sd,dhe->she', x_shard, weight, preferred_element_type=jnp.float32).astype(jnp.bfloat16)

        q_all = project(w_q)
        k_all = project(w_k)
        v_all = project(w_v)
        my_rank = lax.axis_index('cp')
        row_ids = lax.broadcasted_iota(jnp.int32, (block_len, shard_len), 0)
        col_ids = lax.broadcasted_iota(jnp.int32, (block_len, shard_len), 1)
        lo_mask = col_ids[:, :block_len] <= row_ids[:, :block_len]
        hi_mask = col_ids <= row_ids + block_len
        lo_state = online_update(q_all[:block_len], k_all[:block_len], v_all[:block_len], empty_state(n_heads, block_len, head_dim), lo_mask)
        hi_state = online_update(q_all[block_len:], k_all, v_all, empty_state(n_heads, block_len, head_dim), hi_mask)
        start_state = tuple(jnp.concatenate([lo_part, hi_part], axis=1) for lo_part, hi_part in zip(lo_state, hi_state))

        def keys_before(operands):
            k_blk, v_blk, softmax_state = operands
            return online_update(q_all, k_blk[:block_len], v_blk[:block_len], softmax_state, None)

        def keys_after(operands):
            k_blk, v_blk, softmax_state = operands
            upper_state = tuple(piece[:, block_len:] for piece in softmax_state)
            updated = online_update(q_all[block_len:], k_blk, v_blk, upper_state, None)
            return tuple(jnp.concatenate([piece[:, :block_len], fresh], axis=1) for piece, fresh in zip(softmax_state, updated))

        def kv_step(step_idx, loop_carry):
            k_cur, v_cur, softmax_state = loop_carry
            k_cur, v_cur = lax.ppermute((k_cur, v_cur), 'cp', send_perm)
            rank_from = (my_rank - step_idx) % cp_size
            softmax_state = lax.cond(rank_from < my_rank, keys_before, keys_after, (k_cur, v_cur, softmax_state))
            return k_cur, v_cur, softmax_state

        final_carry = lax.fori_loop(1, cp_size, kv_step, (k_all, v_all, start_state))
        final_state = final_carry[2]
        attn_out = (final_state[2] / final_state[1][..., None]).astype(jnp.bfloat16)
        y_part = jnp.einsum('hqe,hed->qd', attn_out, w_o, preferred_element_type=jnp.float32)
        y_loc = lax.psum_scatter(y_part, 'tp', scatter_dimension=0, tiled=True)
        return y_loc.astype(jnp.bfloat16)

    seq_spec = P(('dp', 'cp', 'tp'), None)
    head_spec = P(None, 'tp', None)
    return jax.shard_map(device_fn, mesh=mesh, in_specs=(seq_spec, head_spec, head_spec, head_spec, P('tp', None, None)), out_specs=seq_spec, check_vma=False)
```

profile of v0, /device:TPU:0, one launch (start us, length us, event | category | flops | bytes accessed | tf_op | source)
XLA Modules:
  0.0 98.2 jit_solution(16004361624752528891)
XLA Ops:
  6.6 9.1 %all_gather.3 = bf16[64,3072]{1,0:T(8,128)(2,1)S(1)} all-gather(bf16[32,3072]{1,0:T(8,128)(2,1)} %param.9), channel_id=1, replica_groups=mesh['dp'=1,'tp'=2,'cp'=4] {'tp'}, dimensions={0}, use_global_device_ids=true | all-gather | bytes 589824 | tf_op jit(solution)/shard_map/all_gather | solution.py:32
  15.6 7.1 %fusion.17 = bf16[64,8,256]{2,0,1:T(8,128)(2,1)S(1)} fusion(bf16[3072,8,256]{2,1,0:T(8,128)(2,1)} %param.11, bf16[64,3072]{1,0:T(8,128)(2,1)S(1)} %all_gather.3), kind=kOutput, calls=%fused_computation.30 | convolution fusion | flops 805437440 | bytes 13238272 | tf_op jit(solution)/shard_map/sd,dhe->she/dot_general | solution.py:39
  22.8 2.6 %fusion.23 = bf16[64,8,256]{2,0,1:T(8,128)(2,1)S(1)} fusion(bf16[3072,8,256]{2,1,0:T(8,128)(2,1)S(1)} %copy-done, bf16[64,3072]{1,0:T(8,128)(2,1)S(1)} %all_gather.3), kind=kOutput, calls=%fused_computation.32 | convolution fusion | flops 805437440 | bytes 13238272 | tf_op jit(solution)/shard_map/sd,dhe->she/dot_general | solution.py:39
  25.6 0.3 fusion.48
  26.0 2.6 %fusion.20 = bf16[64,8,256]{2,0,1:T(8,128)(2,1)S(1)} fusion(bf16[3072,8,256]{2,1,0:T(8,128)(2,1)S(1)} %copy-done.1, bf16[64,3072]{1,0:T(8,128)(2,1)S(1)} %all_gather.3), kind=kOutput, calls=%fused_computation.31 | convolution fusion | flops 805437440 | bytes 13238272 | tf_op jit(solution)/shard_map/sd,dhe->she/dot_general | solution.py:39
  29.5 33.0 %while.23 = (s32[]{:T(128)}, bf16[64,8,256]{2,0,1:T(8,128)(2,1)S(1)}, bf16[64,8,256]{2,0,1:T(8,128)(2,1)S(1)}, f32[8,64]{1,0:T(8,128)S(1)}, f32[8,64]{1,0:T(8,12...) while((s32[]{:T(128)}, ...), condition=%wide.region_11.12_spmd, body=%wide.region_4.11_spmd.sunk | while | flops 17139216 | bytes 6126020 | solution.py:70
  29.5 1.8 %collective-permute-start.1 = (bf16[64,8,256]{2,0,1:T(8,128)(2,1)S(1)}, bf16[64,8,256]{2,0,1:T(8,128)(2,1)S(1)}, u32[]{:S(2)}, u32[]{:S(2)}) collective-permute-start(bf16[64,8,256]{2,0,1:T(8,128)(2,1)S(1)} %get-tuple-element.374), channel_id=1, source_target_pairs={{0,1},{1,2},{2,3},{3,0},{4,5},{5,6},{6,7},{7,4}} | collective-permute-start | bytes 786440 | tf_op jit(solution)/shard_map/while/body/eval_jaxpr/ppermute | solution.py:65
  31.3 4.0 %collective-permute-done = bf16[64,8,256]{2,0,1:T(8,128)(2,1)S(1)} collective-permute-done((bf16[64,8,256]{2,0,1:T(8,128)(2,1)S(1)}, bf16[64,8,256]{2,0,1:T(8,128)(2,1)S(1)}, u32[]{:S(2)}, u32[]{:S(2)}) %collective-permute-start) | collective-permute-done | bytes 262176 | tf_op jit(solution)/shard_map/while/body/eval_jaxpr/ppermute | solution.py:65
  35.3 2.8 %collective-permute-done.1 = bf16[64,8,256]{2,0,1:T(8,128)(2,1)S(1)} collective-permute-done((bf16[64,8,256]{2,0,1:T(8,128)(2,1)S(1)}, bf16[64,8,256]{2,0,1:T(8,128)(2,1)S(1)}, u32[]{:S(2)}, u32[]{:S(2)}) %collective-permute-start.1) | collective-permute-done | bytes 262176 | tf_op jit(solution)/shard_map/while/body/eval_jaxpr/ppermute | solution.py:65
  38.1 1.6 %conditional.2 = (f32[8,64]{1,0:T(8,128)}, f32[8,64]{1,0:T(8,128)S(1)}, f32[8,64,256]{2,1,0:T(8,128)S(1)}) conditional(s32[]{:T(128)} %convert_element_type.58, (f32[8,64]{1,0:T(8,128)S(1)}, bf16[64,8,256]{2,0,1:T(8,128)(2,1)S(1)}, bf16[64,8,256]{2,0,1:T(8,128)(2,1)S(1)}, f32[8,64]{1,0:T(8,128)S(1)}, f32[8,64,256]{2,1,0:T(8,128)S(1)}, ...), branch_computations={%region_5.7_spmd, %region_8.10_spmd} | conditional | flops 17139200 | bytes 2975768 | solution.py:67
  38.1 0.3 fusion.46
  39.1 0.7 pad_maximum_fusion.1
  39.7 0.7 copy.44
  40.5 1.0 %collective-permute-start = (bf16[64,8,256]{2,0,1:T(8,128)(2,1)S(1)}, bf16[64,8,256]{2,0,1:T(8,128)(2,1)S(1)}, u32[]{:S(2)}, u32[]{:S(2)}) collective-permute-start(bf16[64,8,256]{2,0,1:T(8,128)(2,1)S(1)} %get-tuple-element.373), channel_id=1, source_target_pairs={{0,1},{1,2},{2,3},{3,0},{4,5},{5,6},{6,7},{7,4}} | collective-permute-start | bytes 786440 | tf_op jit(solution)/shard_map/while/body/eval_jaxpr/ppermute | solution.py:65
  41.5 2.5 %collective-permute-start.1 = (bf16[64,8,256]{2,0,1:T(8,128)(2,1)S(1)}, bf16[64,8,256]{2,0,1:T(8,128)(2,1)S(1)}, u32[]{:S(2)}, u32[]{:S(2)}) collective-permute-start(bf16[64,8,256]{2,0,1:T(8,128)(2,1)S(1)} %get-tuple-element.374), channel_id=1, source_target_pairs={{0,1},{1,2},{2,3},{3,0},{4,5},{5,6},{6,7},{7,4}} | collective-permute-start | bytes 786440 | tf_op jit(solution)/shard_map/while/body/eval_jaxpr/ppermute | solution.py:65
  44.0 2.3 %collective-permute-done = bf16[64,8,256]{2,0,1:T(8,128)(2,1)S(1)} collective-permute-done((bf16[64,8,256]{2,0,1:T(8,128)(2,1)S(1)}, bf16[64,8,256]{2,0,1:T(8,128)(2,1)S(1)}, u32[]{:S(2)}, u32[]{:S(2)}) %collective-permute-start) | collective-permute-done | bytes 262176 | tf_op jit(solution)/shard_map/while/body/eval_jaxpr/ppermute | solution.py:65
  46.3 2.8 %collective-permute-done.1 = bf16[64,8,256]{2,0,1:T(8,128)(2,1)S(1)} collective-permute-done((bf16[64,8,256]{2,0,1:T(8,128)(2,1)S(1)}, bf16[64,8,256]{2,0,1:T(8,128)(2,1)S(1)}, u32[]{:S(2)}, u32[]{:S(2)}) %collective-permute-start.1) | collective-permute-done | bytes 262176 | tf_op jit(solution)/shard_map/while/body/eval_jaxpr/ppermute | solution.py:65
  49.1 1.6 %conditional.2 = (f32[8,64]{1,0:T(8,128)}, f32[8,64]{1,0:T(8,128)S(1)}, f32[8,64,256]{2,1,0:T(8,128)S(1)}) conditional(s32[]{:T(128)} %convert_element_type.58, (f32[8,64]{1,0:T(8,128)S(1)}, bf16[64,8,256]{2,0,1:T(8,128)(2,1)S(1)}, bf16[64,8,256]{2,0,1:T(8,128)(2,1)S(1)}, f32[8,64]{1,0:T(8,128)S(1)}, f32[8,64,256]{2,1,0:T(8,128)S(1)}, ...), branch_computations={%region_5.7_spmd, %region_8.10_spmd} | conditional | flops 17139200 | bytes 2975768 | solution.py:67
  49.1 0.3 fusion.46
  50.1 0.7 pad_maximum_fusion.1
  50.7 0.7 copy.44
  51.5 1.0 %collective-permute-start = (bf16[64,8,256]{2,0,1:T(8,128)(2,1)S(1)}, bf16[64,8,256]{2,0,1:T(8,128)(2,1)S(1)}, u32[]{:S(2)}, u32[]{:S(2)}) collective-permute-start(bf16[64,8,256]{2,0,1:T(8,128)(2,1)S(1)} %get-tuple-element.373), channel_id=1, source_target_pairs={{0,1},{1,2},{2,3},{3,0},{4,5},{5,6},{6,7},{7,4}} | collective-permute-start | bytes 786440 | tf_op jit(solution)/shard_map/while/body/eval_jaxpr/ppermute | solution.py:65
  52.5 4.2 %collective-permute-start.1 = (bf16[64,8,256]{2,0,1:T(8,128)(2,1)S(1)}, bf16[64,8,256]{2,0,1:T(8,128)(2,1)S(1)}, u32[]{:S(2)}, u32[]{:S(2)}) collective-permute-start(bf16[64,8,256]{2,0,1:T(8,128)(2,1)S(1)} %get-tuple-element.374), channel_id=1, source_target_pairs={{0,1},{1,2},{2,3},{3,0},{4,5},{5,6},{6,7},{7,4}} | collective-permute-start | bytes 786440 | tf_op jit(solution)/shard_map/while/body/eval_jaxpr/ppermute | solution.py:65
  56.7 0.6 collective-permute-done
  57.3 2.8 %collective-permute-done.1 = bf16[64,8,256]{2,0,1:T(8,128)(2,1)S(1)} collective-permute-done((bf16[64,8,256]{2,0,1:T(8,128)(2,1)S(1)}, bf16[64,8,256]{2,0,1:T(8,128)(2,1)S(1)}, u32[]{:S(2)}, u32[]{:S(2)}) %collective-permute-start.1) | collective-permute-done | bytes 262176 | tf_op jit(solution)/shard_map/while/body/eval_jaxpr/ppermute | solution.py:65
  60.1 1.6 %conditional.2 = (f32[8,64]{1,0:T(8,128)}, f32[8,64]{1,0:T(8,128)S(1)}, f32[8,64,256]{2,1,0:T(8,128)S(1)}) conditional(s32[]{:T(128)} %convert_element_type.58, (f32[8,64]{1,0:T(8,128)S(1)}, bf16[64,8,256]{2,0,1:T(8,128)(2,1)S(1)}, bf16[64,8,256]{2,0,1:T(8,128)(2,1)S(1)}, f32[8,64]{1,0:T(8,128)S(1)}, f32[8,64,256]{2,1,0:T(8,128)S(1)}, ...), branch_computations={%region_5.7_spmd, %region_8.10_spmd} | conditional | flops 17139200 | bytes 2975768 | solution.py:67
  60.1 0.3 fusion.46
  61.1 0.7 pad_maximum_fusion.1
  61.8 0.7 copy.44
  62.5 7.8 %convolution_bitcast_fusion = f32[64,3072]{1,0:T(8,128)} fusion(bf16[8,256,3072]{2,1,0:T(8,128)(2,1)} %param.13, f32[8,64,256]{2,1,0:T(8,128)S(1)} %get-tuple-element.259, f32[8,64]{1,0:T(8,128)S(1)} %get-tuple-element.260), kind=kOutput, calls=%fused_computation.29 | convolution fusion | flops 805568512 | bytes 13895680 | tf_op jit(solution)/shard_map/hqe,hed->qd/dot_general | solution.py:73
  70.4 19.3 %reduce-scatter.2.cloned.1.call-done = f32[32,3072]{1,0:T(8,128)} async-done(((f32[64,3072]{1,0:T(8,128)}), f32[32,3072]{1,0:T(8,128)}) %reduce-scatter.2.cloned.1.call-update) | async-done | bytes 393232 | tf_op jit(solution)/shard_map/reduce_scatter | solution.py:74
  89.7 1.7 %convert_element_type.43 = bf16[32,3072]{1,0:T(8,128)(2,1)} convert(f32[32,3072]{1,0:T(8,128)} %reduce-scatter.2.cloned.1.call-done) | non-fusion elementwise | flops 98304 | bytes 589824 | tf_op jit(solution)/shard_map/convert_element_type | solution.py:75
  (45 shorter events, 3.3 us)
Async XLA Ops:
  6.5 83.1 %reduce-scatter.2.cloned.1.call-start = ((), (), s32[]{:S(2)}) async-start(), calls=%async_computation.1 | async-start | bytes 1179648 | tf_op jit(solution)/shard_map/reduce_scatter | solution.py:74
  6.5 16.2 %copy-start = (bf16[3072,8,256]{2,1,0:T(8,128)(2,1)S(1)}, bf16[3072,8,256]{2,1,0:T(8,128)(2,1)}, u32[]{:S(2)}) copy-start(bf16[3072,8,256]{2,1,0:T(8,128)(2,1)} %param.10) | copy-start | bytes 37748740
  15.6 10.4 %copy-start.1 = (bf16[3072,8,256]{2,1,0:T(8,128)(2,1)S(1)}, bf16[3072,8,256]{2,1,0:T(8,128)(2,1)}, u32[]{:S(2)}) copy-start(bf16[3072,8,256]{2,1,0:T(8,128)(2,1)} %param.12) | copy-start | bytes 37748740
  29.5 5.8 %collective-permute-start = (bf16[64,8,256]{2,0,1:T(8,128)(2,1)S(1)}, bf16[64,8,256]{2,0,1:T(8,128)(2,1)S(1)}, u32[]{:S(2)}, u32[]{:S(2)}) collective-permute-start(bf16[64,8,256]{2,0,1:T(8,128)(2,1)S(1)} %get-tuple-element.373), channel_id=1, source_target_pairs={{0,1},{1,2},{2,3},{3,0},{4,5},{5,6},{6,7},{7,4}} | collective-permute-start | bytes 786440 | tf_op jit(solution)/shard_map/while/body/eval_jaxpr/ppermute | solution.py:65
  29.5 8.6 %collective-permute-start.1 = (bf16[64,8,256]{2,0,1:T(8,128)(2,1)S(1)}, bf16[64,8,256]{2,0,1:T(8,128)(2,1)S(1)}, u32[]{:S(2)}, u32[]{:S(2)}) collective-permute-start(bf16[64,8,256]{2,0,1:T(8,128)(2,1)S(1)} %get-tuple-element.374), channel_id=1, source_target_pairs={{0,1},{1,2},{2,3},{3,0},{4,5},{5,6},{6,7},{7,4}} | collective-permute-start | bytes 786440 | tf_op jit(solution)/shard_map/while/body/eval_jaxpr/ppermute | solution.py:65
  40.5 5.8 %collective-permute-start = (bf16[64,8,256]{2,0,1:T(8,128)(2,1)S(1)}, bf16[64,8,256]{2,0,1:T(8,128)(2,1)S(1)}, u32[]{:S(2)}, u32[]{:S(2)}) collective-permute-start(bf16[64,8,256]{2,0,1:T(8,128)(2,1)S(1)} %get-tuple-element.373), channel_id=1, source_target_pairs={{0,1},{1,2},{2,3},{3,0},{4,5},{5,6},{6,7},{7,4}} | collective-permute-start | bytes 786440 | tf_op jit(solution)/shard_map/while/body/eval_jaxpr/ppermute | solution.py:65
  41.5 7.6 %collective-permute-start.1 = (bf16[64,8,256]{2,0,1:T(8,128)(2,1)S(1)}, bf16[64,8,256]{2,0,1:T(8,128)(2,1)S(1)}, u32[]{:S(2)}, u32[]{:S(2)}) collective-permute-start(bf16[64,8,256]{2,0,1:T(8,128)(2,1)S(1)} %get-tuple-element.374), channel_id=1, source_target_pairs={{0,1},{1,2},{2,3},{3,0},{4,5},{5,6},{6,7},{7,4}} | collective-permute-start | bytes 786440 | tf_op jit(solution)/shard_map/while/body/eval_jaxpr/ppermute | solution.py:65
  51.5 5.8 %collective-permute-start = (bf16[64,8,256]{2,0,1:T(8,128)(2,1)S(1)}, bf16[64,8,256]{2,0,1:T(8,128)(2,1)S(1)}, u32[]{:S(2)}, u32[]{:S(2)}) collective-permute-start(bf16[64,8,256]{2,0,1:T(8,128)(2,1)S(1)} %get-tuple-element.373), channel_id=1, source_target_pairs={{0,1},{1,2},{2,3},{3,0},{4,5},{5,6},{6,7},{7,4}} | collective-permute-start | bytes 786440 | tf_op jit(solution)/shard_map/while/body/eval_jaxpr/ppermute | solution.py:65
  52.5 7.6 %collective-permute-start.1 = (bf16[64,8,256]{2,0,1:T(8,128)(2,1)S(1)}, bf16[64,8,256]{2,0,1:T(8,128)(2,1)S(1)}, u32[]{:S(2)}, u32[]{:S(2)}) collective-permute-start(bf16[64,8,256]{2,0,1:T(8,128)(2,1)S(1)} %get-tuple-element.374), channel_id=1, source_target_pairs={{0,1},{1,2},{2,3},{3,0},{4,5},{5,6},{6,7},{7,4}} | collective-permute-start | bytes 786440 | tf_op jit(solution)/shard_map/while/body/eval_jaxpr/ppermute | solution.py:65
Sparse Core Ops, SparseCore 0:
  70.5 19.1 reduce-scatter.1
where the time goes:
time: 98.7 us; the launch traced here: 98.2 us
  waiting for transfers between devices  34.7 us (35%)
  matrix products  22.6 us (23%)
  between operations  13.5 us (14%)
  starting transfers between devices  10.5 us (11%)
  blocking collectives  9.05 us (9%)
  other arithmetic  5.38 us (5%)
  local copies, waits for them, and re-layouts  2.24 us (2%)
    reduce_scatter x1, waiting for transfers between devices, device_fn(): y_loc = lax.psum_scatter(y_part, 'tp', scatter_dimension=0, tiled=True)  19.3 us
    ppermute x6, waiting for transfers between devices, kv_step(): k_cur, v_cur = lax.ppermute((k_cur, v_cur), 'cp', send_perm)  15.3 us
    dot_general x3, matrix products, project(): jnp.einsum('sd,dhe->she', x_shard, weight, preferred_element_type=jnp.flo...  12.3 us
    ppermute x6, starting transfers between devices, kv_step(): k_cur, v_cur = lax.ppermute((k_cur, v_cur), 'cp', send_perm)  10.5 us
    all_gather x1, blocking collectives, device_fn(): x_shard = lax.all_gather(x_loc, 'tp', axis=0, tiled=True)  9.05 us
    dot_general x1, matrix products, device_fn(): jnp.einsum('hqe,hed->qd', attn_out, w_o, preferred_element_type=jnp.float32)  7.83 us
    while x9, local copies, waits for them, and re-layouts  2.17 us
    concatenate x6, other arithmetic, keys_after(): jnp.concatenate([piece[:, :block_len], fresh], axis=1)  2.12 us
  transfers between devices with their start and end apart: 7, of which 7 were waited for; matrix products, arithmetic and copies ran while one was open for 0% of the time, Pallas kernels for 0%

commit v1 on v0

v1 whole, which is shorter than its diff:
```python
import functools

import jax
import jax.numpy as jnp
from jax import lax
from jax.experimental import pallas as pl
from jax.experimental.pallas import tpu as pltpu
from jax.sharding import PartitionSpec as P

MESH = pl.DeviceIdType.MESH
BF16 = jnp.bfloat16
F32 = jnp.float32

ROWS = 32
SEQ = 256
D = 3072
E = 256
HC = 4
KB = 512
NK = D // KB
NB = 256
NN = D // NB
NEG = -1e30
OWN_Y, OWN_X, OWN_C, FWD, Y_C, X_C, G_C = range(7)


def kernel(x_hbm, wq_hbm, wk_hbm, wv_hbm, wo_hbm, out_ref,
           xg, raw, wd, wo, qkv, oall, oown, orecv, yown, ysend, yrecv,
           x_sem, w_sem, wo_sem, xs_sem, xr_sem, os_sem, or_sem, ys_sem, yr_sem):
    t = lax.axis_index("tp")
    cp = lax.axis_index("cp")
    xx = cp // 2
    c = cp % 2
    cx = (cp + 2) % 4
    to_y = {"tp": 1 - t}
    to_x = {"cp": cx}
    to_c = {"cp": cp + 1 - 2 * c}

    def block(tt, pp):
        return pp + tt * (7 - 2 * pp)

    own = block(t, cp)
    b_y = block(1 - t, cp)
    b_x = block(t, cx)
    b_g = block(1 - t, cx)

    def x_rows(b, k):
        return xg.at[pl.ds(pl.multiple_of(b * ROWS, ROWS), ROWS), pl.ds(pl.multiple_of(k * KB, KB), KB)]

    x_copy = pltpu.make_async_copy(x_hbm, xg.at[pl.ds(pl.multiple_of(own * ROWS, ROWS), ROWS), :], x_sem)
    x_copy.start()

    def w_copy(m, k, half):
        src = (wq_hbm, wk_hbm, wv_hbm)[m]
        return pltpu.make_async_copy(src.at[k, half, :, :, c], raw.at[m, k, :, :, pl.ds(4 * half, 4)], w_sem.at[m, k, half])

    for k in range(NK):
        for m in range(3):
            for half in range(2):
                w_copy(m, k, half).start()

    def wo_copy():
        return pltpu.make_async_copy(wo_hbm, wo, wo_sem)

    wo_copy().start()

    barrier = pltpu.get_barrier_semaphore()
    for peer in (to_y, to_x, to_c):
        pl.semaphore_signal(barrier, inc=1, device_id=peer, device_id_type=MESH)
    pl.semaphore_wait(barrier, 3)

    def send(kind, k, b, peer):
        return pltpu.make_async_remote_copy(
            src_ref=x_rows(b, k), dst_ref=x_rows(b, k), send_sem=xs_sem.at[kind, k], recv_sem=xr_sem.at[kind, k],
            device_id=peer, device_id_type=MESH)

    x_copy.wait()
    for k in range(NK):
        send(OWN_Y, k, own, to_y).start()
        send(OWN_X, k, own, to_x).start()
    for k in range(NK):
        send(OWN_C, k, own, to_c).start()

    def handle_direct(k):
        send(OWN_Y, k, b_y, to_y).wait_recv()
        if isinstance(k, int):
            even = k % 2 == 0
        send(Y_C, k, b_y, to_c).start()
        if even:
            send(FWD, k, b_y, to_x).start()
        send(OWN_X, k, b_x, to_x).wait_recv()
        send(X_C, k, b_x, to_c).start()
        if not even:
            send(FWD, k, b_x, to_y).start()

    def handle_diag(k):
        send(FWD, k, b_g, to_x).wait_recv()
        send(G_C, k, b_g, to_c).start()

    def deint(m, k):
        for half in range(2):
            w_copy(m, k, half).wait()
        for j in range(2):
            for q in range(4):
                v = jnp.swapaxes(raw[m, k, pl.ds(q * 64, 64), j], 0, 1)
                for half in range(2):
                    for h in range(HC):
                        wd[m * HC + h, pl.ds(k * KB + half * 256 + q * 64, 64), pl.ds(j * 128, 128)] = v[half * 4 + h]

    for k in range(NK):
        for m in range(3):
            deint(m, k)
        if k >= 1:
            handle_direct(k - 1)
        if k >= 3:
            handle_diag(k - 3)
    handle_direct(NK - 1)
    for k in range(NK - 3, NK):
        handle_diag(k)
    p_own = block(t, cp + 1 - 2 * c)
    p_y = block(1 - t, cp + 1 - 2 * c)
    p_cp = (cp + 1 - 2 * c + 2) % 4
    p_x = block(t, p_cp)
    p_g = block(1 - t, p_cp)
    for k in range(NK):
        send(OWN_C, k, p_own, to_c).wait_recv()
        send(Y_C, k, p_y, to_c).wait_recv()
        send(X_C, k, p_x, to_c).wait_recv()
        send(G_C, k, p_g, to_c).wait_recv()

    def project(i, _):
        qkv[i] = jnp.dot(xg[...], wd[i], preferred_element_type=F32).astype(BF16)
        return 0

    lax.fori_loop(0, 3 * HC, project, 0)

    lo0 = pl.multiple_of(xx * 64, 64)
    hi0 = pl.multiple_of(192 - xx * 64, 64)

    def attend(h, start, n_keys):
        q = qkv[h, pl.ds(start, 64), :]
        kk = qkv[HC + h, :n_keys, :]
        vv = qkv[2 * HC + h, :n_keys, :]
        s = lax.dot_general(q, kk, (((1,), (1,)), ((), ())), preferred_element_type=F32) * (E ** -0.5)
        rows = start + lax.broadcasted_iota(jnp.int32, (64, n_keys), 0)
        cols = lax.broadcasted_iota(jnp.int32, (64, n_keys), 1)
        s = jnp.where(cols <= rows, s, NEG)
        m = jnp.max(s, axis=-1, keepdims=True)
        p = jnp.exp(s - m)
        l = jnp.sum(p, axis=-1, keepdims=True)
        o = jnp.dot(p.astype(BF16), vv, preferred_element_type=F32)
        return (o / l).astype(BF16)

    def o_copy(h, part):
        src = 2 * part + (1 - c)
        slot = jnp.where(part == 0, 1 - t, t)
        return pltpu.make_async_remote_copy(
            src_ref=oall.at[src, h], dst_ref=orecv.at[slot, h], send_sem=os_sem.at[part, h], recv_sem=or_sem.at[part, h],
            device_id=to_c, device_id_type=MESH)

    for h in range(HC):
        o_lo = attend(h, lo0, 128)
        o_hi = attend(h, hi0, 256)
        oall[0, h] = o_lo[:32]
        oall[1, h] = o_lo[32:]
        oall[3, h] = o_hi[:32]
        oall[2, h] = o_hi[32:]
        for part in range(2):
            o_copy(h, part).start()
    for h in range(HC):
        oown[1 - t, h] = oall[c, h]
        oown[t, h] = oall[2 + c, h]
    for h in range(HC):
        for part in range(2):
            o_copy(h, part).wait_recv()

    wo_copy().wait()
    mine = pl.multiple_of(c * 1024, 1024)
    other = pl.multiple_of((1 - c) * 1024, 1024)

    def y_copy(n):
        return pltpu.make_async_remote_copy(
            src_ref=ysend.at[n], dst_ref=yrecv.at[n], send_sem=ys_sem.at[n], recv_sem=yr_sem.at[n],
            device_id=to_y, device_id_type=MESH)

    def out_proj(n, _):
        cols = pl.ds(pl.multiple_of(n * NB, NB), NB)
        acc = jnp.zeros((64, NB), F32)
        for h in range(HC):
            a = jnp.concatenate([oown[0, h], oown[1, h]], axis=0)
            acc += jnp.dot(a, wo[pl.ds(mine + h * E, E), cols], preferred_element_type=F32)
        for h in range(HC):
            a = jnp.concatenate([orecv[0, h], orecv[1, h]], axis=0)
            acc += jnp.dot(a, wo[pl.ds(other + h * E, E), cols], preferred_element_type=F32)
        ysend[n] = acc[:32]
        yown[n] = acc[32:]
        y_copy(n).start()
        return 0

    lax.fori_loop(0, NN, out_proj, 0)

    for n in range(NN):
        y_copy(n).wait_recv()
        out_ref[:, n * NB:(n + 1) * NB] = (yown[n] + yrecv[n]).astype(BF16)

    for k in range(NK):
        for kind in range(7):
            send(kind, k, own, to_y).wait_send()
    for h in range(HC):
        for part in range(2):
            o_copy(h, part).wait_send()
    for n in range(NN):
        y_copy(n).wait_send()


def solution(mesh):
    def device_fn(x_loc, w_q, w_k, w_v, w_o):
        def view(w):
            w = w.reshape(NK, 2, 256, 2, HC, 2, 128)
            return w.transpose(0, 1, 2, 5, 3, 4, 6)

        any_spec = pl.BlockSpec(memory_space=pl.ANY)
        dma = pltpu.SemaphoreType.DMA
        return pl.pallas_call(
            kernel,
            out_shape=jax.ShapeDtypeStruct((ROWS, D), BF16),
            in_specs=[any_spec] * 5,
            out_specs=pl.BlockSpec(memory_space=pltpu.VMEM),
            scratch_shapes=[
                pltpu.VMEM((SEQ, D), BF16),
                pltpu.VMEM((3, NK, 256, 2, 8, 128), BF16),
                pltpu.VMEM((3 * HC, D, E), BF16),
                pltpu.VMEM((2 * HC * E, D), BF16),
                pltpu.VMEM((3 * HC, SEQ, E), BF16),
                pltpu.VMEM((4, HC, 32, E), BF16),
                pltpu.VMEM((2, HC, 32, E), BF16),
                pltpu.VMEM((2, HC, 32, E), BF16),
                pltpu.VMEM((NN, 32, NB), F32),
                pltpu.VMEM((NN, 32, NB), F32),
                pltpu.VMEM((NN, 32, NB), F32),
                dma, dma((3, NK, 2)), dma,
                dma((7, NK)), dma((7, NK)),
                dma((2, HC)), dma((2, HC)),
                dma((NN,)), dma((NN,)),
            ],
            compiler_params=pltpu.CompilerParams(
                collective_id=0, has_side_effects=True, vmem_limit_bytes=63 << 20),
            name="mha",
        )(x_loc, view(w_q), view(w_k), view(w_v), w_o.reshape(2 * HC * E, D))

    seq_spec = P(("dp", "cp", "tp"), None)
    head_spec = P(None, "tp", None)
    return jax.shard_map(device_fn, mesh=mesh, in_specs=(seq_spec, head_spec, head_spec, head_spec, P("tp", None, None)), out_specs=seq_spec, check_vma=False)
```

time: 98.7 us -> 45.2 us (0.46)
  Pallas kernels: 0 us -> 43.4 us
  waiting for transfers between devices: 34.7 us -> 0 us
  matrix products: 22.6 us -> 0 us
  between operations: 13.5 us -> 0.01 us
  starting transfers between devices: 10.5 us -> 0 us
  blocking collectives: 9.05 us -> 0 us
  other arithmetic: 5.38 us -> 0 us
    pallas_call x0 -> x1, Pallas kernels: none -> 43.4 us  [device_fn(): pl.pallas_call(kernel, out_shape=jax.ShapeDtypeStruct((ROWS, D), BF16), i...]
    dot_general x14 -> x0, matrix products: 22.6 us -> none  [the longest x3 12.3 us: project(): jnp.einsum('sd,dhe->she', x_shard, weight, preferred_element_type=jnp.flo...]
    reduce_scatter x1 -> x0, waiting for transfers between devices: 19.3 us -> none  [device_fn(): y_loc = lax.psum_scatter(y_part, 'tp', scatter_dimension=0, tiled=True)]
    ppermute x6 -> x0, waiting for transfers between devices: 15.3 us -> none  [kv_step(): k_cur, v_cur = lax.ppermute((k_cur, v_cur), 'cp', send_perm)]
    ppermute x6 -> x0, starting transfers between devices: 10.5 us -> none  [kv_step(): k_cur, v_cur = lax.ppermute((k_cur, v_cur), 'cp', send_perm)]
    all_gather x1 -> x0, blocking collectives: 9.05 us -> none  [device_fn(): x_shard = lax.all_gather(x_loc, 'tp', axis=0, tiled=True)]
    concatenate x9 -> x0, other arithmetic: 2.3 us -> none  [the longest x6 2.12 us: keys_after(): jnp.concatenate([piece[:, :block_len], fresh], axis=1)]
    while x9 -> x0, local copies, waits for them, and re-layouts: 2.17 us -> none
  transfers between devices with their start and end apart: 7 -> 0, of which waited for: 7 -> 0; matrix products, arithmetic and copies ran while one was open for 0% -> 0% of each run, Pallas kernels for 0% -> 0%
where the time goes in v1:
time: 45.2 us; the launch traced here: 45.1 us
  Pallas kernels  43.4 us (96%)
  local copies, waits for them, and re-layouts  1.62 us (4%)
    pallas_call x1, Pallas kernels, device_fn(): pl.pallas_call(kernel, out_shape=jax.ShapeDtypeStruct((ROWS, D), BF16), i...  43.4 us
    unnamed x1, local copies, waits for them, and re-layouts  1.62 us

profile of v1, /device:TPU:0, one launch (start us, length us, event | category | flops | bytes accessed | tf_op | source)
XLA Modules:
  0.0 45.1 jit_solution(11966305879793209750)
XLA Ops:
  0.0 43.4 %mha.1 = bf16[32,3072]{1,0:T(8,128)(2,1)} custom-call(bf16[32,3072]{1,0:T(8,128)(2,1)} %x_hbm.1, bf16[6,2,256,2,2,4,128]{6,5,4,3,2,1,0:T(4,128)(2,1)} %bitcast.10, bf16[6,2,256,2,2,4,128]{6,5,4,3,2,1,0:T(4,128)(2,1)} %bitcast.11, bf16[6,2,256,2,2,4,128]{6,5,4,3,2,1,0:T(4,128)(2,1)} %bitcast.12, bf16[2048,3072]{1,0:T(8,128)(2,1)} %bitcast.13), custom_call_target="tpu_custom_call" | custom-call | tf_op jit(solution)/shard_map/mha/pallas_call | solution.py:224
  43.4 1.6 %copy.7 = bf16[32,3072]{1,0:T(8,128)(2,1)} copy(bf16[32,3072]{1,0:T(8,128)(2,1)} %mha.1) | data formatting | bytes 393216

commit v2 on v1

--- a/solution.py
+++ b/solution.py
@@ -18,6 +18,7 @@
 HC = 4
 KB = 512
 NK = D // KB
+DH = D // 2
 NB = 256
 NN = D // NB
 NEG = -1e30
@@ -25,7 +26,7 @@
 
 
 def kernel(x_hbm, wq_hbm, wk_hbm, wv_hbm, wo_hbm, out_ref,
-           xg, raw, wd, wo, qkv, oall, oown, orecv, yown, ysend, yrecv,
+           xg, raw, wd, wo, xq, qb, kvacc, kv, oall, oown, orecv, yown, ysend, yrecv,
            x_sem, w_sem, wo_sem, xs_sem, xr_sem, os_sem, or_sem, ys_sem, yr_sem):
     t = lax.axis_index("tp")
     cp = lax.axis_index("cp")
@@ -54,27 +55,27 @@
         src = (wq_hbm, wk_hbm, wv_hbm)[m]
         return pltpu.make_async_copy(src.at[k, half, :, :, c], raw.at[m, k, :, :, pl.ds(4 * half, 4)], w_sem.at[m, k, half])
 
+    def wo_copy():
+        return pltpu.make_async_copy(wo_hbm, wo, wo_sem)
+
+    barrier = pltpu.get_barrier_semaphore()
+    for peer in (to_y, to_x, to_c):
+        pl.semaphore_signal(barrier, inc=1, device_id=peer, device_id_type=MESH)
+    with jax.named_scope("xwait"):
+        x_copy.wait()
     for k in range(NK):
         for m in range(3):
             for half in range(2):
                 w_copy(m, k, half).start()
-
-    def wo_copy():
-        return pltpu.make_async_copy(wo_hbm, wo, wo_sem)
-
     wo_copy().start()
-
-    barrier = pltpu.get_barrier_semaphore()
-    for peer in (to_y, to_x, to_c):
-        pl.semaphore_signal(barrier, inc=1, device_id=peer, device_id_type=MESH)
-    pl.semaphore_wait(barrier, 3)
+    with jax.named_scope("barrier"):
+        pl.semaphore_wait(barrier, 3)
 
     def send(kind, k, b, peer):
         return pltpu.make_async_remote_copy(
             src_ref=x_rows(b, k), dst_ref=x_rows(b, k), send_sem=xs_sem.at[kind, k], recv_sem=xr_sem.at[kind, k],
             device_id=peer, device_id_type=MESH)
 
-    x_copy.wait()
     for k in range(NK):
         send(OWN_Y, k, own, to_y).start()
         send(OWN_X, k, own, to_x).start()
@@ -83,8 +84,7 @@
 
     def handle_direct(k):
         send(OWN_Y, k, b_y, to_y).wait_recv()
-        if isinstance(k, int):
-            even = k % 2 == 0
+        even = k % 2 == 0
         send(Y_C, k, b_y, to_c).start()
         if even:
             send(FWD, k, b_y, to_x).start()
@@ -107,49 +107,73 @@
                     for h in range(HC):
                         wd[m * HC + h, pl.ds(k * KB + half * 256 + q * 64, 64), pl.ds(j * 128, 128)] = v[half * 4 + h]
 
-    for k in range(NK):
-        for m in range(3):
-            deint(m, k)
-        if k >= 1:
-            handle_direct(k - 1)
-        if k >= 3:
-            handle_diag(k - 3)
-    handle_direct(NK - 1)
-    for k in range(NK - 3, NK):
-        handle_diag(k)
+    lo0 = pl.multiple_of(xx * 64, 64)
+    hi0 = pl.multiple_of(192 - xx * 64, 64)
     p_own = block(t, cp + 1 - 2 * c)
     p_y = block(1 - t, cp + 1 - 2 * c)
     p_cp = (cp + 1 - 2 * c + 2) % 4
     p_x = block(t, p_cp)
     p_g = block(1 - t, p_cp)
-    for k in range(NK):
-        send(OWN_C, k, p_own, to_c).wait_recv()
-        send(Y_C, k, p_y, to_c).wait_recv()
-        send(X_C, k, p_x, to_c).wait_recv()
-        send(G_C, k, p_g, to_c).wait_recv()
-
-    def project(i, _):
-        qkv[i] = jnp.dot(xg[...], wd[i], preferred_element_type=F32).astype(BF16)
+
+    for k in range(NK):
+        with jax.named_scope(f"deint{k}"):
+            for m in range(3):
+                deint(m, k)
+        if k >= 2:
+            with jax.named_scope(f"direct{k - 2}"):
+                handle_direct(k - 2)
+    for k in range(NK - 2, NK):
+        with jax.named_scope(f"direct{k}"):
+            handle_direct(k)
+    with jax.named_scope("qwait"):
+        for k in range(NK):
+            send(OWN_C, k, p_own, to_c).wait_recv()
+            send(Y_C, k, p_y, to_c).wait_recv()
+    xq[:64] = xg[pl.ds(lo0, 64), :]
+    xq[64:] = xg[pl.ds(hi0, 64), :]
+    for h in range(2):
+        with jax.named_scope(f"qproj{h}"):
+            for i in (2 * h, 2 * h + 1):
+                qb[i] = jnp.dot(xq[...], wd[i], preferred_element_type=F32).astype(BF16)
+        with jax.named_scope(f"diag{h}"):
+            for k in range(3 * h, 3 * h + 3):
+                handle_diag(k)
+
+    with jax.named_scope("kvwait0"):
+        for k in range(3):
+            send(X_C, k, p_x, to_c).wait_recv()
+            send(G_C, k, p_g, to_c).wait_recv()
+
+    def kv_first(i, _):
+        kvacc[i] = jnp.dot(xg[:, :DH], wd[HC + i, :DH], preferred_element_type=F32)
         return 0
 
-    lax.fori_loop(0, 3 * HC, project, 0)
-
-    lo0 = pl.multiple_of(xx * 64, 64)
-    hi0 = pl.multiple_of(192 - xx * 64, 64)
-
-    def attend(h, start, n_keys):
-        q = qkv[h, pl.ds(start, 64), :]
-        kk = qkv[HC + h, :n_keys, :]
-        vv = qkv[2 * HC + h, :n_keys, :]
-        s = lax.dot_general(q, kk, (((1,), (1,)), ((), ())), preferred_element_type=F32) * (E ** -0.5)
+    with jax.named_scope("kv0"):
+        lax.fori_loop(0, 2 * HC, kv_first, 0, unroll=4)
+    with jax.named_scope("kvwait1"):
+        for k in range(3, NK):
+            send(X_C, k, p_x, to_c).wait_recv()
+            send(G_C, k, p_g, to_c).wait_recv()
+
+    def kv_second(i, _):
+        kv[i] = (kvacc[i] + jnp.dot(xg[:, DH:], wd[HC + i, DH:], preferred_element_type=F32)).astype(BF16)
+        return 0
+
+    with jax.named_scope("kv1"):
+        lax.fori_loop(0, 2 * HC, kv_second, 0, unroll=4)
+
+    def attend(part, start, n_keys):
+        heads = range(HC)
         rows = start + lax.broadcasted_iota(jnp.int32, (64, n_keys), 0)
-        cols = lax.broadcasted_iota(jnp.int32, (64, n_keys), 1)
-        s = jnp.where(cols <= rows, s, NEG)
-        m = jnp.max(s, axis=-1, keepdims=True)
-        p = jnp.exp(s - m)
-        l = jnp.sum(p, axis=-1, keepdims=True)
-        o = jnp.dot(p.astype(BF16), vv, preferred_element_type=F32)
-        return (o / l).astype(BF16)
+        seen = lax.broadcasted_iota(jnp.int32, (64, n_keys), 1) <= rows
+        s = [lax.dot_general(qb[h, part * 64:part * 64 + 64, :], kv[h, :n_keys, :], (((1,), (1,)), ((), ())), preferred_element_type=F32)
+             for h in heads]
+        s = [jnp.where(seen, v * (E ** -0.5), NEG) for v in s]
+        m = [jnp.max(v, axis=-1, keepdims=True) for v in s]
+        p = [jnp.exp(v - w) for v, w in zip(s, m)]
+        l = [jnp.sum(v, axis=-1, keepdims=True) for v in p]
+        o = [jnp.dot(p[h].astype(BF16), kv[HC + h, :n_keys, :], preferred_element_type=F32) for h in heads]
+        return [(o[h] / l[h]).astype(BF16) for h in heads]
 
     def o_copy(h, part):
         src = 2 * part + (1 - c)
@@ -158,23 +182,26 @@
             src_ref=oall.at[src, h], dst_ref=orecv.at[slot, h], send_sem=os_sem.at[part, h], recv_sem=or_sem.at[part, h],
             device_id=to_c, device_id_type=MESH)
 
+    with jax.named_scope("attn"):
+        o_lo = attend(0, lo0, 128)
+        o_hi = attend(1, hi0, 256)
+        for h in range(HC):
+            oall[0, h] = o_lo[h][:32]
+            oall[1, h] = o_lo[h][32:]
+            oall[3, h] = o_hi[h][:32]
+            oall[2, h] = o_hi[h][32:]
     for h in range(HC):
-        o_lo = attend(h, lo0, 128)
-        o_hi = attend(h, hi0, 256)
-        oall[0, h] = o_lo[:32]
-        oall[1, h] = o_lo[32:]
-        oall[3, h] = o_hi[:32]
-        oall[2, h] = o_hi[32:]
         for part in range(2):
             o_copy(h, part).start()
     for h in range(HC):
         oown[1 - t, h] = oall[c, h]
         oown[t, h] = oall[2 + c, h]
-    for h in range(HC):
-        for part in range(2):
-            o_copy(h, part).wait_recv()
-
-    wo_copy().wait()
+    with jax.named_scope("owait"):
+        for h in range(HC):
+            for part in range(2):
+                o_copy(h, part).wait_recv()
+    with jax.named_scope("wowait"):
+        wo_copy().wait()
     mine = pl.multiple_of(c * 1024, 1024)
     other = pl.multiple_of((1 - c) * 1024, 1024)
 
@@ -197,10 +224,12 @@
         y_copy(n).start()
         return 0
 
-    lax.fori_loop(0, NN, out_proj, 0)
+    with jax.named_scope('outproj'):
+        lax.fori_loop(0, NN, out_proj, 0)
 
     for n in range(NN):
-        y_copy(n).wait_recv()
+        with jax.named_scope(f"yw{n}"):
+            y_copy(n).wait_recv()
         out_ref[:, n * NB:(n + 1) * NB] = (yown[n] + yrecv[n]).astype(BF16)
 
     for k in range(NK):
@@ -223,7 +252,7 @@
         dma = pltpu.SemaphoreType.DMA
         return pl.pallas_call(
             kernel,
-            out_shape=jax.ShapeDtypeStruct((ROWS, D), BF16),
+            out_shape=pltpu.VMEM((ROWS, D), BF16),
             in_specs=[any_spec] * 5,
             out_specs=pl.BlockSpec(memory_space=pltpu.VMEM),
             scratch_shapes=[
@@ -231,7 +260,10 @@
                 pltpu.VMEM((3, NK, 256, 2, 8, 128), BF16),
                 pltpu.VMEM((3 * HC, D, E), BF16),
                 pltpu.VMEM((2 * HC * E, D), BF16),
-                pltpu.VMEM((3 * HC, SEQ, E), BF16),
+                pltpu.VMEM((128, D), BF16),
+                pltpu.VMEM((HC, 128, E), BF16),
+                pltpu.VMEM((2 * HC, SEQ, E), F32),
+                pltpu.VMEM((2 * HC, SEQ, E), BF16),
                 pltpu.VMEM((4, HC, 32, E), BF16),
                 pltpu.VMEM((2, HC, 32, E), BF16),
                 pltpu.VMEM((2, HC, 32, E), BF16),

time: 45.2 us -> 32.6 us (0.72)
  Pallas kernels: 43.4 us -> 31.8 us
  local copies, waits for them, and re-layouts: 1.62 us -> 0.68 us
    pallas_call x1, Pallas kernels: 43.4 us -> 31.8 us  [device_fn(): pl.pallas_call(kernel, out_shape=pltpu.VMEM((ROWS, D), BF16), in_specs=[a...]
    unnamed x1, local copies, waits for them, and re-layouts: 1.62 us -> 0.68 us
where the time goes in v2:
time: 32.6 us; the launch traced here: 32.5 us
  Pallas kernels  31.8 us (98%)
  local copies, waits for them, and re-layouts  0.68 us (2%)
    pallas_call x1, Pallas kernels, device_fn(): pl.pallas_call(kernel, out_shape=pltpu.VMEM((ROWS, D), BF16), in_specs=[a...  31.8 us
    unnamed x1, local copies, waits for them, and re-layouts  0.68 us

profile of v2, /device:TPU:0, one launch (start us, length us, event | category | flops | bytes accessed | tf_op | source)
XLA Modules:
  0.0 32.5 jit_solution(17185668276039494601)
XLA Ops:
  0.0 31.8 %mha.1 = bf16[32,3072]{1,0:T(8,128)(2,1)S(1)} custom-call(bf16[32,3072]{1,0:T(8,128)(2,1)} %x_hbm.1, bf16[6,2,256,2,2,4,128]{6,5,4,3,2,1,0:T(4,128)(2,1)} %bitcast.10, bf16[6,2,256,2,2,4,128]{6,5,4,3,2,1,0:T(4,128)(2,1)} %bitcast.11, bf16[6,2,256,2,2,4,128]{6,5,4,3,2,1,0:T(4,128)(2,1)} %bitcast.12, bf16[2048,3072]{1,0:T(8,128)(2,1)} %bitcast.13), custom_call_target="tpu_custom_call" | custom-call | tf_op jit(solution)/shard_map/mha/pallas_call | solution.py:253
  31.8 0.7 %copy.7 = bf16[32,3072]{1,0:T(8,128)(2,1)} copy(bf16[32,3072]{1,0:T(8,128)(2,1)S(1)} %mha.1) | data formatting | bytes 393216

commit v3 on v2

v3 whole, which is shorter than its diff:
```python
import functools

import jax
import jax.numpy as jnp
from jax import lax
from jax.experimental import pallas as pl
from jax.experimental.pallas import tpu as pltpu
from jax.sharding import PartitionSpec as P

MESH = pl.DeviceIdType.MESH
BF16 = jnp.bfloat16
F32 = jnp.float32

ROWS = 32
SEQ = 256
D = 3072
E = 256
HC = 4
KB = 512
NK = D // KB
NB = 256
NN = D // NB
NEG = -1e30
OWN_Y, OWN_X, OWN_C, FWD, Y_C, X_C, G_C = range(7)


def kernel(x_hbm, wq_hbm, wk_hbm, wv_hbm, wo_hbm, out_ref,
           xg, raw, wd, wo, qacc, qb, kvacc, kv, oall, oown, orecv, yown, ysend, yrecv,
           x_sem, w_sem, wo_sem, xs_sem, xr_sem, os_sem, or_sem, ys_sem, yr_sem):
    t = lax.axis_index("tp")
    cp = lax.axis_index("cp")
    xx = cp // 2
    c = cp % 2
    cx = (cp + 2) % 4
    to_y = {"tp": 1 - t}
    to_x = {"cp": cx}
    to_c = {"cp": cp + 1 - 2 * c}

    def block(tt, pp):
        return pp + tt * (7 - 2 * pp)

    own = block(t, cp)
    b_y = block(1 - t, cp)
    b_x = block(t, cx)
    b_g = block(1 - t, cx)

    def x_rows(b, k):
        return xg.at[pl.ds(pl.multiple_of(b * ROWS, ROWS), ROWS), pl.ds(pl.multiple_of(k * KB, KB), KB)]

    x_copy = pltpu.make_async_copy(x_hbm, xg.at[pl.ds(pl.multiple_of(own * ROWS, ROWS), ROWS), :], x_sem)
    x_copy.start()

    def w_copy(m, k, half):
        src = (wq_hbm, wk_hbm, wv_hbm)[m]
        return pltpu.make_async_copy(src.at[k, half, :, :, c], raw.at[m, k, :, :, pl.ds(4 * half, 4)], w_sem.at[3 * k + m if k < 2 else 4 + k])

    def wo_copy():
        return pltpu.make_async_copy(wo_hbm, wo, wo_sem)

    barrier = pltpu.get_barrier_semaphore()
    for peer in (to_y, to_x, to_c):
        pl.semaphore_signal(barrier, inc=1, device_id=peer, device_id_type=MESH)
    with jax.named_scope("xwait"):
        x_copy.wait()
    for k in range(NK):
        for m in range(3):
            for half in range(2):
                w_copy(m, k, half).start()
    wo_copy().start()
    with jax.named_scope("barrier"):
        pl.semaphore_wait(barrier, 3)

    def group(kind, k):
        return {OWN_Y: k, OWN_X: k, FWD: 6 + k // 2, OWN_C: 9 + k // 2, Y_C: 9 + k // 2, X_C: 12 + k // 2, G_C: 12 + k // 2}[kind]

    def send(kind, k, b, peer):
        pltpu.make_async_remote_copy(
            src_ref=x_rows(b, k), dst_ref=x_rows(b, k), send_sem=xs_sem, recv_sem=xr_sem.at[group(kind, k)],
            device_id=peer, device_id_type=MESH).start()

    def arrived(kind, k, pieces):
        whole = xg.at[:ROWS * pieces, :KB]
        pltpu.make_async_remote_copy(
            src_ref=whole, dst_ref=whole, send_sem=xs_sem, recv_sem=xr_sem.at[group(kind, k)],
            device_id=to_c, device_id_type=MESH).wait_recv()

    for k in range(NK):
        send(OWN_Y, k, own, to_y)
        send(OWN_X, k, own, to_x)
    for k in range(NK):
        send(OWN_C, k, own, to_c)

    def handle_direct(k):
        with jax.named_scope(f"direct{k}"):
            arrived(OWN_Y, k, 2)
            if k % 2 == 0:
                send(FWD, k, b_y, to_x)
            else:
                send(FWD, k, b_x, to_y)
            send(Y_C, k, b_y, to_c)
            send(X_C, k, b_x, to_c)

    def handle_diag(k):
        with jax.named_scope(f"diag{k}"):
            arrived(FWD, k, 2)
            send(G_C, k, b_g, to_c)
            send(G_C, k + 1, b_g, to_c)

    def weights_here(m, k):
        if k < 2:
            pltpu.make_async_copy(raw.at[m, k], raw.at[m, k], w_sem.at[3 * k + m]).wait()
        elif m == 0:
            pltpu.make_async_copy(raw.at[:, k], raw.at[:, k], w_sem.at[4 + k]).wait()

    def deint(m, k, piece):
        j, q = piece // 4, piece % 4
        v = jnp.swapaxes(raw[m, k, pl.ds(q * 64, 64), j], 0, 1)
        for half in range(2):
            for h in range(HC):
                wd[m * HC + h, pl.ds(k * KB + half * 256 + q * 64, 64), pl.ds(j * 128, 128)] = v[half * 4 + h]

    lo0 = pl.multiple_of(xx * 64, 64)
    hi0 = pl.multiple_of(192 - xx * 64, 64)

    def q_part(part, h):
        cols = slice(part * 2 * KB, (part + 1) * 2 * KB)
        xq = jnp.concatenate([xg[pl.ds(lo0, 64), cols], xg[pl.ds(hi0, 64), cols]], axis=0)
        q = jnp.dot(xq, wd[h, cols], preferred_element_type=F32)
        if part > 0:
            q = qacc[h] + q
        if part < 2:
            qacc[h] = q
        else:
            qb[h] = q.astype(BF16)

    def step(name, weights, part=None):
        with jax.named_scope(name):
            for m, k in weights:
                weights_here(m, k)
            if part is not None:
                arrived(OWN_C, 2 * part, 4)
            pieces = [(m, k, piece) for m, k in weights for piece in range(8)]
            dots = list(range(HC)) if part is not None else []
            for i, (m, k, piece) in enumerate(pieces):
                if dots and i * HC >= len(pieces) * (HC - len(dots)):
                    q_part(part, dots.pop(0))
                deint(m, k, piece)
            for h in dots:
                q_part(part, h)

    for k in range(2):
        for m in range(3):
            step(f"s{k}{m}", [(m, k)])
    step("s20", [(0, 2)])
    handle_direct(0)
    step("s21", [(1, 2), (2, 2)])
    handle_direct(1)
    step("s30", [(0, 3), (1, 3)])
    handle_direct(2)
    step("s32", [(2, 3), (0, 4)])
    handle_direct(3)
    step("s41", [(1, 4), (2, 4)], 0)
    handle_direct(4)
    step("s50", [(0, 5), (1, 5)])
    handle_direct(5)
    step("s52", [(2, 5)], 1)
    handle_diag(0)
    step("q2", [], 2)
    handle_diag(2)

    for part in range(3):
        cols = slice(part * 2 * KB, (part + 1) * 2 * KB)
        with jax.named_scope(f"kvwait{part}"):
            arrived(X_C, 2 * part, 4)

        def kv_part(i, _, part=part, cols=cols):
            y = jnp.dot(xg[:, cols], wd[HC + i, cols], preferred_element_type=F32)
            if part > 0:
                y = kvacc[i] + y
            if part < 2:
                kvacc[i] = y
            else:
                kv[i] = y.astype(BF16)
            return 0

        with jax.named_scope(f"kv{part}"):
            lax.fori_loop(0, 2 * HC, kv_part, 0, unroll=True)
        if part == 0:
            handle_diag(4)

    def attend(part, start, n_keys):
        heads = range(HC)
        rows = start + lax.broadcasted_iota(jnp.int32, (64, n_keys), 0)
        seen = lax.broadcasted_iota(jnp.int32, (64, n_keys), 1) <= rows
        s = [lax.dot_general(qb[h, part * 64:part * 64 + 64, :], kv[h, :n_keys, :], (((1,), (1,)), ((), ())), preferred_element_type=F32)
             for h in heads]
        s = [jnp.where(seen, v * (E ** -0.5), NEG) for v in s]
        m = [jnp.max(v, axis=-1, keepdims=True) for v in s]
        p = [jnp.exp(v - w) for v, w in zip(s, m)]
        l = [jnp.sum(v, axis=-1, keepdims=True) for v in p]
        o = [jnp.dot(p[h].astype(BF16), kv[HC + h, :n_keys, :], preferred_element_type=F32) for h in heads]
        return [(o[h] / l[h]).astype(BF16) for h in heads]

    def o_send(part):
        src = 2 * part + (1 - c)
        slot = 1 - t if part == 0 else t
        pltpu.make_async_remote_copy(
            src_ref=oall.at[src], dst_ref=orecv.at[slot], send_sem=os_sem, recv_sem=or_sem,
            device_id=to_c, device_id_type=MESH).start()

    def o_all():
        return pltpu.make_async_remote_copy(
            src_ref=orecv, dst_ref=orecv, send_sem=os_sem, recv_sem=or_sem, device_id=to_c, device_id_type=MESH)

    with jax.named_scope("attn"):
        o_lo = attend(0, lo0, 128)
        o_hi = attend(1, hi0, 256)
        for h in range(HC):
            oall[0, h] = o_lo[h][:32]
            oall[1, h] = o_lo[h][32:]
            oall[3, h] = o_hi[h][:32]
            oall[2, h] = o_hi[h][32:]
    for part in range(2):
        o_send(part)
    for h in range(HC):
        oown[1 - t, h] = oall[c, h]
        oown[t, h] = oall[2 + c, h]
    with jax.named_scope("owait"):
        o_all().wait_recv()
    with jax.named_scope("wowait"):
        wo_copy().wait()
    mine = pl.multiple_of(c * 1024, 1024)
    other = pl.multiple_of((1 - c) * 1024, 1024)

    def y_send(n):
        pltpu.make_async_remote_copy(
            src_ref=ysend.at[n], dst_ref=yrecv.at[n], send_sem=ys_sem, recv_sem=yr_sem.at[n // 6 + n // 9 + n // 11],
            device_id=to_y, device_id_type=MESH).start()

    def y_arrived(i, first, last):
        some = yrecv.at[first:last]
        pltpu.make_async_remote_copy(
            src_ref=some, dst_ref=some, send_sem=ys_sem, recv_sem=yr_sem.at[i], device_id=to_y, device_id_type=MESH).wait_recv()

    def out_proj(n, _):
        cols = pl.ds(pl.multiple_of(n * NB, NB), NB)
        acc = jnp.zeros((64, NB), F32)
        for h in range(HC):
            a = jnp.concatenate([oown[0, h], oown[1, h]], axis=0)
            acc += jnp.dot(a, wo[pl.ds(mine + h * E, E), cols], preferred_element_type=F32)
        for h in range(HC):
            a = jnp.concatenate([orecv[0, h], orecv[1, h]], axis=0)
            acc += jnp.dot(a, wo[pl.ds(other + h * E, E), cols], preferred_element_type=F32)
        ysend[n] = acc[:32]
        yown[n] = acc[32:]
        y_send(n)
        return 0

    with jax.named_scope('outproj'):
        lax.fori_loop(0, NN, out_proj, 0)

    for i, (first, last) in enumerate(((0, 6), (6, 9), (9, 11), (11, 12))):
        with jax.named_scope(f"yw{i}"):
            y_arrived(i, first, last)
        for n in range(first, last):
            out_ref[:, n * NB:(n + 1) * NB] = (yown[n] + yrecv[n]).astype(BF16)

    sent = xg.at[:7 * ROWS]
    pltpu.make_async_remote_copy(
        src_ref=sent, dst_ref=sent, send_sem=xs_sem, recv_sem=xr_sem.at[0], device_id=to_c, device_id_type=MESH).wait_send()
    o_all().wait_send()
    pltpu.make_async_remote_copy(
        src_ref=ysend, dst_ref=ysend, send_sem=ys_sem, recv_sem=yr_sem.at[0], device_id=to_y, device_id_type=MESH).wait_send()


def solution(mesh):
    def device_fn(x_loc, w_q, w_k, w_v, w_o):
        def view(w):
            w = w.reshape(NK, 2, 256, 2, HC, 2, 128)
            return w.transpose(0, 1, 2, 5, 3, 4, 6)

        any_spec = pl.BlockSpec(memory_space=pl.ANY)
        dma = pltpu.SemaphoreType.DMA
        return pl.pallas_call(
            kernel,
            out_shape=pltpu.VMEM((ROWS, D), BF16),
            in_specs=[any_spec] * 5,
            out_specs=pl.BlockSpec(memory_space=pltpu.VMEM),
            scratch_shapes=[
                pltpu.VMEM((SEQ, D), BF16),
                pltpu.VMEM((3, NK, 256, 2, 8, 128), BF16),
                pltpu.VMEM((3 * HC, D, E), BF16),
                pltpu.VMEM((2 * HC * E, D), BF16),
                pltpu.VMEM((HC, 128, E), F32),
                pltpu.VMEM((HC, 128, E), BF16),
                pltpu.VMEM((2 * HC, SEQ, E), F32),
                pltpu.VMEM((2 * HC, SEQ, E), BF16),
                pltpu.VMEM((4, HC, 32, E), BF16),
                pltpu.VMEM((2, HC, 32, E), BF16),
                pltpu.VMEM((2, HC, 32, E), BF16),
                pltpu.VMEM((NN, 32, NB), F32),
                pltpu.VMEM((NN, 32, NB), F32),
                pltpu.VMEM((NN, 32, NB), F32),
                dma, dma((10,)), dma,
                dma, dma((15,)),
                dma, dma,
                dma, dma((4,)),
            ],
            compiler_params=pltpu.CompilerParams(
                collective_id=0, has_side_effects=True, vmem_limit_bytes=63 << 20),
            name="mha",
        )(x_loc, view(w_q), view(w_k), view(w_v), w_o.reshape(2 * HC * E, D))

    seq_spec = P(("dp", "cp", "tp"), None)
    head_spec = P(None, "tp", None)
    return jax.shard_map(device_fn, mesh=mesh, in_specs=(seq_spec, head_spec, head_spec, head_spec, P("tp", None, None)), out_specs=seq_spec, check_vma=False)
```

time: 32.6 us -> 29.8 us (0.914)
  Pallas kernels: 31.8 us -> 29 us
    pallas_call x1, Pallas kernels: 31.8 us -> 29 us  [device_fn(): pl.pallas_call(kernel, out_shape=pltpu.VMEM((ROWS, D), BF16), in_specs=[a...]
where the time goes in v3:
time: 29.8 us; the launch traced here: 29.7 us
  Pallas kernels  29 us (97%)
  local copies, waits for them, and re-layouts  0.68 us (2%)
    pallas_call x1, Pallas kernels, device_fn(): pl.pallas_call(kernel, out_shape=pltpu.VMEM((ROWS, D), BF16), in_specs=[a...  29 us
    unnamed x1, local copies, waits for them, and re-layouts  0.68 us

profile of v3, /device:TPU:0, one launch (start us, length us, event | category | flops | bytes accessed | tf_op | source)
XLA Modules:
  0.0 29.7 jit_solution(10066065081561589741)
XLA Ops:
  0.0 29.0 %mha.1 = bf16[32,3072]{1,0:T(8,128)(2,1)S(1)} custom-call(bf16[32,3072]{1,0:T(8,128)(2,1)} %x_hbm.1, bf16[6,2,256,2,2,4,128]{6,5,4,3,2,1,0:T(4,128)(2,1)} %bitcast.10, bf16[6,2,256,2,2,4,128]{6,5,4,3,2,1,0:T(4,128)(2,1)} %bitcast.11, bf16[6,2,256,2,2,4,128]{6,5,4,3,2,1,0:T(4,128)(2,1)} %bitcast.12, bf16[2048,3072]{1,0:T(8,128)(2,1)} %bitcast.13), custom_call_target="tpu_custom_call" | custom-call | tf_op jit(solution)/shard_map/mha/pallas_call | solution.py:284
  29.0 0.7 %copy.7 = bf16[32,3072]{1,0:T(8,128)(2,1)} copy(bf16[32,3072]{1,0:T(8,128)(2,1)S(1)} %mha.1) | data formatting | bytes 393216

commit v4 on v3

v4 whole, which is shorter than its diff:
```python
import functools

import jax
import jax.numpy as jnp
from jax import lax
from jax.experimental import pallas as pl
from jax.experimental.pallas import tpu as pltpu
from jax.sharding import PartitionSpec as P

MESH = pl.DeviceIdType.MESH
BF16 = jnp.bfloat16
F32 = jnp.float32

ROWS = 32
SEQ = 256
D = 3072
E = 256
HC = 4
KB = 512
NK = D // KB
NB = 256
NN = D // NB
NEG = -1e30
YO = (0, 2, 4, 1, 3, 5)
XO = (1, 3, 5, 0, 2, 4)
OWN_Y, OWN_X, OWN_C, FWD, Y_C, X_C, G_C = range(7)


def kernel(x_hbm, wq_hbm, wk_hbm, wv_hbm, wo_hbm, out_ref,
           xg, raw, wd, wo, qacc, qb, kvacc, kv, oall, orecv, yown, ysend, yrecv,
           x_sem, w_sem, wo_sem, xs_sem, xr_sem, os_sem, or_sem, ys_sem, yr_sem):
    t = lax.axis_index("tp")
    cp = lax.axis_index("cp")
    xx = cp // 2
    c = cp % 2
    pc = cp + 1 - 2 * c
    to_c = {"cp": pc}
    to_y = {"tp": 1 - t, "cp": pc}
    to_x = {"cp": (pc + 2) % 4}

    def block(tt, pp):
        return pp + tt * (7 - 2 * pp)

    own = block(t, cp)
    b_y = block(1 - t, pc)
    b_x = block(t, (pc + 2) % 4)
    b_g = block(1 - t, (cp + 2) % 4)

    def x_rows(b, k):
        return xg.at[pl.ds(pl.multiple_of(b * ROWS, ROWS), ROWS), pl.ds(pl.multiple_of(k * KB, KB), KB)]

    x_copy = pltpu.make_async_copy(x_hbm, xg.at[pl.ds(pl.multiple_of(own * ROWS, ROWS), ROWS), :], x_sem)
    x_copy.start()

    def w_copy(m, k, half):
        src = (wq_hbm, wk_hbm, wv_hbm)[m]
        return pltpu.make_async_copy(src.at[k, half, :, :, c], raw.at[m, k, :, :, pl.ds(4 * half, 4)], w_sem.at[3 * k + m])

    def wo_copy():
        return pltpu.make_async_copy(wo_hbm, wo, wo_sem)

    barrier = pltpu.get_barrier_semaphore()
    for peer in (to_y, to_x, to_c):
        pl.semaphore_signal(barrier, inc=1, device_id=peer, device_id_type=MESH)
    with jax.named_scope("xwait"):
        x_copy.wait()
    for k in range(NK):
        for m in range(3):
            for half in range(2):
                w_copy(m, k, half).start()
    with jax.named_scope("barrier"):
        pl.semaphore_wait(barrier, 3)

    def group(kind, k):
        at = {OWN_Y: YO.index(k), OWN_X: XO.index(k), FWD: 6 + k // 2, X_C: 12 + k // 2, G_C: 12 + k // 2}
        return at.get(kind, 9 + YO.index(k) // 2)

    def send(kind, k, b, peer):
        pltpu.make_async_remote_copy(
            src_ref=x_rows(b, k), dst_ref=x_rows(b, k), send_sem=xs_sem, recv_sem=xr_sem.at[group(kind, k)],
            device_id=peer, device_id_type=MESH).start()

    def arrived(kind, k, pieces):
        whole = xg.at[:ROWS * pieces, :KB]
        pltpu.make_async_remote_copy(
            src_ref=whole, dst_ref=whole, send_sem=xs_sem, recv_sem=xr_sem.at[group(kind, k)],
            device_id=to_c, device_id_type=MESH).wait_recv()

    for i in range(NK):
        send(OWN_Y, YO[i], own, to_y)
        send(OWN_X, XO[i], own, to_x)
    for i in range(NK):
        send(OWN_C, YO[i], own, to_c)

    def handle_direct(i):
        with jax.named_scope(f"direct{i}"):
            arrived(OWN_Y, YO[i], 2)
            if i < 3:
                send(FWD, YO[i], b_y, to_x)
                send(FWD, XO[i], b_x, to_y)
            send(Y_C, YO[i], b_y, to_c)
            send(X_C, XO[i], b_x, to_c)

    def handle_diag(k):
        with jax.named_scope(f"diag{k}"):
            arrived(FWD, k, 2)
            send(G_C, k, b_g, to_c)
            send(G_C, k + 1, b_g, to_c)

    def weights_here(m, k):
        pltpu.make_async_copy(raw.at[m, k], raw.at[m, k], w_sem.at[3 * k + m]).wait()

    def deint(m, k, piece):
        j, q = piece // 4, piece % 4
        v = jnp.swapaxes(raw[m, k, pl.ds(q * 64, 64), j], 0, 1)
        for half in range(2):
            for h in range(HC):
                wd[m * HC + h, pl.ds(k * KB + half * 256 + q * 64, 64), pl.ds(j * 128, 128)] = v[half * 4 + h]

    lo0 = pl.multiple_of(xx * 64, 64)
    hi0 = pl.multiple_of(192 - xx * 64, 64)

    def q_part(part, h):
        q = None
        for k in YO[2 * part:2 * part + 2]:
            cols = slice(k * KB, (k + 1) * KB)
            xq = jnp.concatenate([xg[pl.ds(lo0, 64), cols], xg[pl.ds(hi0, 64), cols]], axis=0)
            z = jnp.dot(xq, wd[h, cols], preferred_element_type=F32)
            q = z if q is None else q + z
        if part > 0:
            q = qacc[h] + q
        if part < 2:
            qacc[h] = q
        else:
            qb[h] = q.astype(BF16)

    def step(name, weights, part=None):
        with jax.named_scope(name):
            for m, k in weights:
                weights_here(m, k)
            if part is not None:
                arrived(OWN_C, YO[2 * part], 4)
            pieces = [(m, k, piece) for m, k in weights for piece in range(8)]
            dots = list(range(HC)) if part is not None else []
            for i, (m, k, piece) in enumerate(pieces):
                if dots and i * HC >= len(pieces) * (HC - len(dots)):
                    q_part(part, dots.pop(0))
                deint(m, k, piece)
            for h in dots:
                q_part(part, h)

    def steps(first, last):
        for i in range(first, last):
            step(f"s{i // 3}{i % 3}", [(i % 3, i // 3)])

    first_chip = jnp.logical_and(t == 0, xx == 0)

    def schedule(marks):
        done = 0
        for i, mark in enumerate(marks):
            steps(done, mark)
            done = mark
            if mark == 18 and i == NK - 1:
                step("q0", [], 0)
            handle_direct(i)
        if done < 18:
            steps(done, 18)
            step("q0", [], 0)

    @pl.when(first_chip)
    def _():
        schedule((10, 12, 14, 16, 18, 18))

    @pl.when(jnp.logical_not(first_chip))
    def _():
        schedule((7, 9, 11, 13, 15, 17))

    handle_diag(0)
    step("q1", [], 1)
    handle_diag(2)
    step("q2", [], 2)

    def kv_part(part):
        cols = slice(part * 2 * KB, (part + 1) * 2 * KB)
        with jax.named_scope(f"kvwait{part}"):
            arrived(X_C, 2 * part, 4)
        with jax.named_scope(f"kv{part}"):
            for i in range(2 * HC):
                y = jnp.dot(xg[:, cols], wd[HC + i, cols], preferred_element_type=F32)
                if part > 0:
                    y = kvacc[i] + y
                if part < 2:
                    kvacc[i] = y
                else:
                    kv[i] = y.astype(BF16)

    wo_copy().start()
    kv_part(0)
    handle_diag(4)
    kv_part(1)
    kv_part(2)

    def attend(part):
        start = pl.multiple_of(lo0 + part * (hi0 - lo0), 64)
        heads = range(HC)
        rows = start + lax.broadcasted_iota(jnp.int32, (64, SEQ), 0)
        seen = lax.broadcasted_iota(jnp.int32, (64, SEQ), 1) <= rows
        s = [lax.dot_general(qb[h, pl.ds(pl.multiple_of(part * 64, 64), 64), :], kv[h], (((1,), (1,)), ((), ())),
                             preferred_element_type=F32) for h in heads]
        s = [jnp.where(seen, v * (E ** -0.5), NEG) for v in s]
        m = [jnp.max(v, axis=-1, keepdims=True) for v in s]
        p = [jnp.exp(v - w) for v, w in zip(s, m)]
        l = [jnp.sum(v, axis=-1, keepdims=True) for v in p]
        o = [jnp.dot(p[h].astype(BF16), kv[HC + h], preferred_element_type=F32) for h in heads]
        for h in heads:
            z = (o[h] / l[h]).astype(BF16)
            oall[2 * part, h] = z[:32]
            oall[2 * part + 1, h] = z[32:]

    def o_rows(part, core):
        return oall.at[2 * part + (core + part - 2 * core * part)]

    def core_of(core, slot):
        return 1 - core if slot == 0 else core

    def o_send(part, slot):
        pltpu.make_async_remote_copy(
            src_ref=o_rows(part, core_of(1 - c, slot)), dst_ref=orecv.at[slot], send_sem=os_sem, recv_sem=or_sem.at[slot],
            device_id=to_c, device_id_type=MESH).start()

    def o_arrived(slot):
        pltpu.make_async_remote_copy(
            src_ref=orecv.at[slot], dst_ref=orecv.at[slot], send_sem=os_sem, recv_sem=or_sem.at[slot],
            device_id=to_c, device_id_type=MESH).wait_recv()

    parts = (1 - t, t)
    mine = pl.multiple_of(c * 1024, 1024)
    other = pl.multiple_of((1 - c) * 1024, 1024)

    def y_part(slot, n):
        cols = pl.ds(pl.multiple_of(n * NB, NB), NB)
        acc = jnp.zeros((ROWS, NB), F32)
        for h in range(HC):
            acc += jnp.dot(o_rows(parts[slot], core_of(c, slot))[h], wo[pl.ds(mine + h * E, E), cols], preferred_element_type=F32)
        for h in range(HC):
            acc += jnp.dot(orecv[slot, h], wo[pl.ds(other + h * E, E), cols], preferred_element_type=F32)
        return acc

    def y_send(n):
        pltpu.make_async_remote_copy(
            src_ref=ysend.at[n], dst_ref=yrecv.at[n], send_sem=ys_sem, recv_sem=yr_sem.at[n // 6 + n // 9 + n // 11],
            device_id=to_y, device_id_type=MESH).start()

    def y_arrived(i, first, last):
        some = yrecv.at[first:last]
        pltpu.make_async_remote_copy(
            src_ref=some, dst_ref=some, send_sem=ys_sem, recv_sem=yr_sem.at[i], device_id=to_y, device_id_type=MESH).wait_recv()

    with jax.named_scope("attn0"):
        attend(parts[0])
    o_send(parts[0], 0)
    with jax.named_scope("attn1"):
        attend(parts[1])
    o_send(parts[1], 1)
    with jax.named_scope("wowait"):
        wo_copy().wait()
    with jax.named_scope("owait0"):
        o_arrived(0)

    def out_peer(n, _):
        ysend[n] = y_part(0, n)
        y_send(n)
        return 0

    with jax.named_scope("outproj0"):
        lax.fori_loop(0, NN, out_peer, 0)
    with jax.named_scope("owait1"):
        o_arrived(1)

    def out_own(n, _):
        yown[n] = y_part(1, n)
        return 0

    with jax.named_scope("outproj1"):
        lax.fori_loop(0, NN, out_own, 0)

    for i, (first, last) in enumerate(((0, 6), (6, 9), (9, 11), (11, 12))):
        with jax.named_scope(f"yw{i}"):
            y_arrived(i, first, last)
        for n in range(first, last):
            out_ref[:, n * NB:(n + 1) * NB] = (yown[n] + yrecv[n]).astype(BF16)

    sent = xg.at[:7 * ROWS]
    pltpu.make_async_remote_copy(
        src_ref=sent, dst_ref=sent, send_sem=xs_sem, recv_sem=xr_sem.at[0], device_id=to_c, device_id_type=MESH).wait_send()
    pltpu.make_async_remote_copy(
        src_ref=orecv, dst_ref=orecv, send_sem=os_sem, recv_sem=or_sem.at[0], device_id=to_c, device_id_type=MESH).wait_send()
    pltpu.make_async_remote_copy(
        src_ref=ysend, dst_ref=ysend, send_sem=ys_sem, recv_sem=yr_sem.at[0], device_id=to_y, device_id_type=MESH).wait_send()


def solution(mesh):
    def device_fn(x_loc, w_q, w_k, w_v, w_o):
        def view(w):
            w = w.reshape(NK, 2, 256, 2, HC, 2, 128)
            return w.transpose(0, 1, 2, 5, 3, 4, 6)

        any_spec = pl.BlockSpec(memory_space=pl.ANY)
        dma = pltpu.SemaphoreType.DMA
        return pl.pallas_call(
            kernel,
            out_shape=pltpu.VMEM((ROWS, D), BF16),
            in_specs=[any_spec] * 5,
            out_specs=pl.BlockSpec(memory_space=pltpu.VMEM),
            scratch_shapes=[
                pltpu.VMEM((SEQ, D), BF16),
                pltpu.VMEM((3, NK, 256, 2, 8, 128), BF16),
                pltpu.VMEM((3 * HC, D, E), BF16),
                pltpu.VMEM((2 * HC * E, D), BF16),
                pltpu.VMEM((HC, 128, E), F32),
                pltpu.VMEM((HC, 128, E), BF16),
                pltpu.VMEM((2 * HC, SEQ, E), F32),
                pltpu.VMEM((2 * HC, SEQ, E), BF16),
                pltpu.VMEM((4, HC, 32, E), BF16),
                pltpu.VMEM((2, HC, 32, E), BF16),
                pltpu.VMEM((NN, 32, NB), F32),
                pltpu.VMEM((NN, 32, NB), F32),
                pltpu.VMEM((NN, 32, NB), F32),
                dma, dma((18,)), dma,
                dma, dma((15,)),
                dma, dma((2,)),
                dma, dma((4,)),
            ],
            compiler_params=pltpu.CompilerParams(
                collective_id=0, has_side_effects=True, vmem_limit_bytes=63 << 20),
            name="mha",
        )(x_loc, view(w_q), view(w_k), view(w_v), w_o.reshape(2 * HC * E, D))

    seq_spec = P(("dp", "cp", "tp"), None)
    head_spec = P(None, "tp", None)
    return jax.shard_map(device_fn, mesh=mesh, in_specs=(seq_spec, head_spec, head_spec, head_spec, P("tp", None, None)), out_specs=seq_spec, check_vma=False)
```

time: 29.8 us -> 28.6 us (0.960)
  Pallas kernels: 29 us -> 27.8 us
    pallas_call x1, Pallas kernels: 29 us -> 27.8 us  [device_fn(): pl.pallas_call(kernel, out_shape=pltpu.VMEM((ROWS, D), BF16), in_specs=[a...]
where the time goes in v4:
time: 28.6 us; the launch traced here: 28.5 us
  Pallas kernels  27.8 us (97%)
  local copies, waits for them, and re-layouts  0.68 us (2%)
    pallas_call x1, Pallas kernels, device_fn(): pl.pallas_call(kernel, out_shape=pltpu.VMEM((ROWS, D), BF16), in_specs=[a...  27.8 us
    unnamed x1, local copies, waits for them, and re-layouts  0.68 us

profile of v4, /device:TPU:0, one launch (start us, length us, event | category | flops | bytes accessed | tf_op | source)
XLA Modules:
  0.0 28.5 jit_solution(8814767420682689888)
XLA Ops:
  0.0 27.8 %mha.1 = bf16[32,3072]{1,0:T(8,128)(2,1)S(1)} custom-call(bf16[32,3072]{1,0:T(8,128)(2,1)} %x_hbm.1, bf16[6,2,256,2,2,4,128]{6,5,4,3,2,1,0:T(4,128)(2,1)} %bitcast.10, bf16[6,2,256,2,2,4,128]{6,5,4,3,2,1,0:T(4,128)(2,1)} %bitcast.11, bf16[6,2,256,2,2,4,128]{6,5,4,3,2,1,0:T(4,128)(2,1)} %bitcast.12, bf16[2048,3072]{1,0:T(8,128)(2,1)} %bitcast.13), custom_call_target="tpu_custom_call" | custom-call | tf_op jit(solution)/shard_map/mha/pallas_call | solution.py:310
  27.9 0.7 %copy.7 = bf16[32,3072]{1,0:T(8,128)(2,1)} copy(bf16[32,3072]{1,0:T(8,128)(2,1)S(1)} %mha.1) | data formatting | bytes 393216

commit v5 on v4

--- a/solution.py
+++ b/solution.py
@@ -21,14 +21,15 @@
 NB = 256
 NN = D // NB
 NEG = -1e30
+RR = 2
 YO = (0, 2, 4, 1, 3, 5)
 XO = (1, 3, 5, 0, 2, 4)
 OWN_Y, OWN_X, OWN_C, FWD, Y_C, X_C, G_C = range(7)
 
 
 def kernel(x_hbm, wq_hbm, wk_hbm, wv_hbm, wo_hbm, out_ref,
-           xg, raw, wd, wo, qacc, qb, kvacc, kv, oall, orecv, yown, ysend, yrecv,
-           x_sem, w_sem, wo_sem, xs_sem, xr_sem, os_sem, or_sem, ys_sem, yr_sem):
+           xg, raw, wd, wo, qacc, qb, kvacc, kv, oall, orecv, yown, ysend, yrecv, yfwd,
+           w_sem, xs_sem, xr_sem, os_sem, or_sem, ys_sem, yr_sem, yf_sem):
     t = lax.axis_index("tp")
     cp = lax.axis_index("cp")
     xx = cp // 2
@@ -49,21 +50,25 @@
     def x_rows(b, k):
         return xg.at[pl.ds(pl.multiple_of(b * ROWS, ROWS), ROWS), pl.ds(pl.multiple_of(k * KB, KB), KB)]
 
-    x_copy = pltpu.make_async_copy(x_hbm, xg.at[pl.ds(pl.multiple_of(own * ROWS, ROWS), ROWS), :], x_sem)
-    x_copy.start()
+    def x_copy(k):
+        return pltpu.make_async_copy(x_hbm.at[:, pl.ds(k * KB, KB)], x_rows(own, k), w_sem.at[k])
+
+    for k in range(NK):
+        x_copy(k).start()
 
     def w_copy(m, k, half):
         src = (wq_hbm, wk_hbm, wv_hbm)[m]
         return pltpu.make_async_copy(src.at[k, half, :, :, c], raw.at[m, k, :, :, pl.ds(4 * half, 4)], w_sem.at[3 * k + m])
 
     def wo_copy():
-        return pltpu.make_async_copy(wo_hbm, wo, wo_sem)
+        return pltpu.make_async_copy(wo_hbm, wo, w_sem.at[0])
 
     barrier = pltpu.get_barrier_semaphore()
     for peer in (to_y, to_x, to_c):
         pl.semaphore_signal(barrier, inc=1, device_id=peer, device_id_type=MESH)
     with jax.named_scope("xwait"):
-        x_copy.wait()
+        for k in range(NK):
+            x_copy(k).wait()
     for k in range(NK):
         for m in range(3):
             for half in range(2):
@@ -237,14 +242,45 @@
     mine = pl.multiple_of(c * 1024, 1024)
     other = pl.multiple_of((1 - c) * 1024, 1024)
 
-    def y_part(slot, n):
+    def y_half(slot, n, far):
         cols = pl.ds(pl.multiple_of(n * NB, NB), NB)
         acc = jnp.zeros((ROWS, NB), F32)
         for h in range(HC):
-            acc += jnp.dot(o_rows(parts[slot], core_of(c, slot))[h], wo[pl.ds(mine + h * E, E), cols], preferred_element_type=F32)
-        for h in range(HC):
-            acc += jnp.dot(orecv[slot, h], wo[pl.ds(other + h * E, E), cols], preferred_element_type=F32)
+            if far:
+                acc += jnp.dot(orecv[slot, h], wo[pl.ds(other + h * E, E), cols], preferred_element_type=F32)
+            else:
+                acc += jnp.dot(o_rows(parts[slot], core_of(c, slot))[h], wo[pl.ds(mine + h * E, E), cols], preferred_element_type=F32)
         return acc
+
+    def y_part(slot, n):
+        return y_half(slot, n, False) + y_half(slot, n, True)
+
+    def from_chip(n):
+        return jnp.logical_and(jnp.logical_and(t == 1, xx == 0), c <= 1 - n)
+
+    def by_chip(n):
+        return jnp.logical_and(jnp.logical_and(t == 0, xx == 1), c <= 1 - n)
+
+    def y_round(n):
+        return pltpu.make_async_remote_copy(
+            src_ref=ysend.at[n], dst_ref=yfwd.at[n], send_sem=ys_sem, recv_sem=yf_sem.at[n],
+            device_id={"tp": 1 - t, "cp": (cp + 2) % 4}, device_id_type=MESH)
+
+    def y_forward(n):
+        return pltpu.make_async_remote_copy(
+            src_ref=yfwd.at[n], dst_ref=yrecv.at[n], send_sem=yf_sem.at[RR + n], recv_sem=yr_sem.at[4 + n],
+            device_id=to_x, device_id_type=MESH)
+
+    def y_first(n):
+        @pl.when(from_chip(n))
+        def _():
+            y_round(n).start()
+
+        @pl.when(jnp.logical_not(from_chip(n)))
+        def _():
+            pltpu.make_async_remote_copy(
+                src_ref=ysend.at[n], dst_ref=yrecv.at[n], send_sem=ys_sem, recv_sem=yr_sem.at[4 + n],
+                device_id=to_y, device_id_type=MESH).start()
 
     def y_send(n):
         pltpu.make_async_remote_copy(
@@ -264,6 +300,8 @@
     o_send(parts[1], 1)
     with jax.named_scope("wowait"):
         wo_copy().wait()
+    with jax.named_scope("early"):
+        yown[0] = y_half(0, RR, False)
     with jax.named_scope("owait0"):
         o_arrived(0)
 
@@ -273,7 +311,18 @@
         return 0
 
     with jax.named_scope("outproj0"):
-        lax.fori_loop(0, NN, out_peer, 0)
+        ysend[RR] = yown[0] + y_half(0, RR, True)
+        y_send(RR)
+        for n in range(RR):
+            ysend[n] = y_part(0, n)
+            y_first(n)
+        lax.fori_loop(RR + 1, NN, out_peer, 0)
+    with jax.named_scope("forward"):
+        for n in range(RR):
+            @pl.when(by_chip(n))
+            def _(n=n):
+                y_round(n).wait_recv()
+                y_forward(n).start()
     with jax.named_scope("owait1"):
         o_arrived(1)
 
@@ -284,10 +333,15 @@
     with jax.named_scope("outproj1"):
         lax.fori_loop(0, NN, out_own, 0)
 
-    for i, (first, last) in enumerate(((0, 6), (6, 9), (9, 11), (11, 12))):
+    for i, (first, last) in enumerate(((RR, 6), (6, 9), (9, 11), (11, 12))):
         with jax.named_scope(f"yw{i}"):
             y_arrived(i, first, last)
-        for n in range(first, last):
+        if i == 2:
+            for n in range(RR):
+                y_arrived(4 + n, n, n + 1)
+        for n in range(first if i != 2 else 0, last):
+            if i == 2 and RR <= n < first:
+                continue
             out_ref[:, n * NB:(n + 1) * NB] = (yown[n] + yrecv[n]).astype(BF16)
 
     sent = xg.at[:7 * ROWS]
@@ -297,6 +351,11 @@
         src_ref=orecv, dst_ref=orecv, send_sem=os_sem, recv_sem=or_sem.at[0], device_id=to_c, device_id_type=MESH).wait_send()
     pltpu.make_async_remote_copy(
         src_ref=ysend, dst_ref=ysend, send_sem=ys_sem, recv_sem=yr_sem.at[0], device_id=to_y, device_id_type=MESH).wait_send()
+
+    for n in range(RR):
+        @pl.when(by_chip(n))
+        def _(n=n):
+            y_forward(n).wait_send()
 
 
 def solution(mesh):
@@ -326,10 +385,11 @@
                 pltpu.VMEM((NN, 32, NB), F32),
                 pltpu.VMEM((NN, 32, NB), F32),
                 pltpu.VMEM((NN, 32, NB), F32),
-                dma, dma((18,)), dma,
+                pltpu.VMEM((RR, 32, NB), F32),
+                dma((18,)),
                 dma, dma((15,)),
                 dma, dma((2,)),
-                dma, dma((4,)),
+                dma, dma((4 + RR,)), dma((2 * RR,)),
             ],
             compiler_params=pltpu.CompilerParams(
                 collective_id=0, has_side_effects=True, vmem_limit_bytes=63 << 20),

time: 28.6 us -> 27.7 us (0.969)
  Pallas kernels: 27.8 us -> 26.9 us
    pallas_call x1, Pallas kernels: 27.8 us -> 26.9 us  [device_fn(): pl.pallas_call(kernel, out_shape=pltpu.VMEM((ROWS, D), BF16), in_specs=[a...]
where the time goes in v5:
time: 27.7 us; the launch traced here: 27.6 us
  Pallas kernels  26.9 us (97%)
  local copies, waits for them, and re-layouts  0.68 us (2%)
    pallas_call x1, Pallas kernels, device_fn(): pl.pallas_call(kernel, out_shape=pltpu.VMEM((ROWS, D), BF16), in_specs=[a...  26.9 us
    unnamed x1, local copies, waits for them, and re-layouts  0.68 us

profile of v5, /device:TPU:0, one launch (start us, length us, event | category | flops | bytes accessed | tf_op | source)
XLA Modules:
  0.0 27.6 jit_solution(8747580600712380529)
XLA Ops:
  0.0 26.9 %mha.1 = bf16[32,3072]{1,0:T(8,128)(2,1)S(1)} custom-call(bf16[32,3072]{1,0:T(8,128)(2,1)} %x_hbm.1, bf16[6,2,256,2,2,4,128]{6,5,4,3,2,1,0:T(4,128)(2,1)} %bitcast.10, bf16[6,2,256,2,2,4,128]{6,5,4,3,2,1,0:T(4,128)(2,1)} %bitcast.11, bf16[6,2,256,2,2,4,128]{6,5,4,3,2,1,0:T(4,128)(2,1)} %bitcast.12, bf16[2048,3072]{1,0:T(8,128)(2,1)} %bitcast.13), custom_call_target="tpu_custom_call" | custom-call | tf_op jit(solution)/shard_map/mha/pallas_call | solution.py:369
  26.9 0.7 %copy.7 = bf16[32,3072]{1,0:T(8,128)(2,1)} copy(bf16[32,3072]{1,0:T(8,128)(2,1)S(1)} %mha.1) | data formatting | bytes 393216

commit v6 on v5

--- a/solution.py
+++ b/solution.py
@@ -175,15 +175,25 @@
     @pl.when(first_chip)
     def _():
         schedule((10, 12, 14, 16, 18, 18))
-
-    @pl.when(jnp.logical_not(first_chip))
+        step("q1", [], 1)
+        handle_diag(0)
+        step("q2", [], 2)
+        handle_diag(2)
+
+    def others(marks):
+        schedule(marks)
+        handle_diag(0)
+        step("q1", [], 1)
+        handle_diag(2)
+        step("q2", [], 2)
+
+    @pl.when(jnp.logical_and(jnp.logical_not(first_chip), c == 0))
     def _():
-        schedule((7, 9, 11, 13, 15, 17))
-
-    handle_diag(0)
-    step("q1", [], 1)
-    handle_diag(2)
-    step("q2", [], 2)
+        others((7, 9, 11, 13, 15, 17))
+
+    @pl.when(jnp.logical_and(jnp.logical_not(first_chip), c == 1))
+    def _():
+        others((9, 11, 13, 15, 17, 18))
 
     def kv_part(part):
         cols = slice(part * 2 * KB, (part + 1) * 2 * KB)
@@ -205,18 +215,18 @@
     kv_part(1)
     kv_part(2)
 
-    def attend(part):
-        start = pl.multiple_of(lo0 + part * (hi0 - lo0), 64)
+    def attend(part, n_keys):
+        start = lo0 if part == 0 else hi0
         heads = range(HC)
-        rows = start + lax.broadcasted_iota(jnp.int32, (64, SEQ), 0)
-        seen = lax.broadcasted_iota(jnp.int32, (64, SEQ), 1) <= rows
-        s = [lax.dot_general(qb[h, pl.ds(pl.multiple_of(part * 64, 64), 64), :], kv[h], (((1,), (1,)), ((), ())),
+        rows = start + lax.broadcasted_iota(jnp.int32, (64, n_keys), 0)
+        seen = lax.broadcasted_iota(jnp.int32, (64, n_keys), 1) <= rows
+        s = [lax.dot_general(qb[h, part * 64:part * 64 + 64, :], kv[h, :n_keys, :], (((1,), (1,)), ((), ())),
                              preferred_element_type=F32) for h in heads]
         s = [jnp.where(seen, v * (E ** -0.5), NEG) for v in s]
         m = [jnp.max(v, axis=-1, keepdims=True) for v in s]
         p = [jnp.exp(v - w) for v, w in zip(s, m)]
         l = [jnp.sum(v, axis=-1, keepdims=True) for v in p]
-        o = [jnp.dot(p[h].astype(BF16), kv[HC + h], preferred_element_type=F32) for h in heads]
+        o = [jnp.dot(p[h].astype(BF16), kv[HC + h, :n_keys, :], preferred_element_type=F32) for h in heads]
         for h in heads:
             z = (o[h] / l[h]).astype(BF16)
             oall[2 * part, h] = z[:32]
@@ -255,11 +265,8 @@
     def y_part(slot, n):
         return y_half(slot, n, False) + y_half(slot, n, True)
 
-    def from_chip(n):
-        return jnp.logical_and(jnp.logical_and(t == 1, xx == 0), c <= 1 - n)
-
-    def by_chip(n):
-        return jnp.logical_and(jnp.logical_and(t == 0, xx == 1), c <= 1 - n)
+    from_chip = jnp.logical_and(jnp.logical_and(t == 1, xx == 0), c == 1)
+    by_chip = jnp.logical_and(jnp.logical_and(t == 0, xx == 1), c == 1)
 
     def y_round(n):
         return pltpu.make_async_remote_copy(
@@ -272,11 +279,11 @@
             device_id=to_x, device_id_type=MESH)
 
     def y_first(n):
-        @pl.when(from_chip(n))
+        @pl.when(from_chip)
         def _():
             y_round(n).start()
 
-        @pl.when(jnp.logical_not(from_chip(n)))
+        @pl.when(jnp.logical_not(from_chip))
         def _():
             pltpu.make_async_remote_copy(
                 src_ref=ysend.at[n], dst_ref=yrecv.at[n], send_sem=ys_sem, recv_sem=yr_sem.at[4 + n],
@@ -292,12 +299,20 @@
         pltpu.make_async_remote_copy(
             src_ref=some, dst_ref=some, send_sem=ys_sem, recv_sem=yr_sem.at[i], device_id=to_y, device_id_type=MESH).wait_recv()
 
-    with jax.named_scope("attn0"):
-        attend(parts[0])
-    o_send(parts[0], 0)
-    with jax.named_scope("attn1"):
-        attend(parts[1])
-    o_send(parts[1], 1)
+    def attend_both(order):
+        for slot, part in enumerate(order):
+            with jax.named_scope(f"attn{slot}"):
+                attend(part, 128 if part == 0 else SEQ)
+            o_send(part, slot)
+
+    @pl.when(t == 1)
+    def _():
+        attend_both((0, 1))
+
+    @pl.when(t == 0)
+    def _():
+        attend_both((1, 0))
+
     with jax.named_scope("wowait"):
         wo_copy().wait()
     with jax.named_scope("early"):
@@ -319,7 +334,7 @@
         lax.fori_loop(RR + 1, NN, out_peer, 0)
     with jax.named_scope("forward"):
         for n in range(RR):
-            @pl.when(by_chip(n))
+            @pl.when(by_chip)
             def _(n=n):
                 y_round(n).wait_recv()
                 y_forward(n).start()
@@ -353,7 +368,7 @@
         src_ref=ysend, dst_ref=ysend, send_sem=ys_sem, recv_sem=yr_sem.at[0], device_id=to_y, device_id_type=MESH).wait_send()
 
     for n in range(RR):
-        @pl.when(by_chip(n))
+        @pl.when(by_chip)
         def _(n=n):
             y_forward(n).wait_send()
 

time: 27.7 us -> 27.7 us (level)
  no operation moved by 1% of the time
where the time goes in v6:
time: 27.7 us; the launch traced here: 27.5 us
  Pallas kernels  26.9 us (97%)
  local copies, waits for them, and re-layouts  0.68 us (2%)
    pallas_call x1, Pallas kernels, device_fn(): pl.pallas_call(kernel, out_shape=pltpu.VMEM((ROWS, D), BF16), in_specs=[a...  26.9 us
    unnamed x1, local copies, waits for them, and re-layouts  0.68 us

profile of v6, /device:TPU:0, one launch (start us, length us, event | category | flops | bytes accessed | tf_op | source)
XLA Modules:
  0.0 27.5 jit_solution(13392545337110655254)
XLA Ops:
  0.0 26.9 %mha.1 = bf16[32,3072]{1,0:T(8,128)(2,1)S(1)} custom-call(bf16[32,3072]{1,0:T(8,128)(2,1)} %x_hbm.1, bf16[6,2,256,2,2,4,128]{6,5,4,3,2,1,0:T(4,128)(2,1)} %bitcast.10, bf16[6,2,256,2,2,4,128]{6,5,4,3,2,1,0:T(4,128)(2,1)} %bitcast.11, bf16[6,2,256,2,2,4,128]{6,5,4,3,2,1,0:T(4,128)(2,1)} %bitcast.12, bf16[2048,3072]{1,0:T(8,128)(2,1)} %bitcast.13), custom_call_target="tpu_custom_call" | custom-call | tf_op jit(solution)/shard_map/mha/pallas_call | solution.py:384
  26.9 0.7 %copy.7 = bf16[32,3072]{1,0:T(8,128)(2,1)} copy(bf16[32,3072]{1,0:T(8,128)(2,1)S(1)} %mha.1) | data formatting | bytes 393216

commit v7 on v6

--- a/solution.py
+++ b/solution.py
@@ -175,6 +175,7 @@
     @pl.when(first_chip)
     def _():
         schedule((10, 12, 14, 16, 18, 18))
+        wo_copy().start()
         step("q1", [], 1)
         handle_diag(0)
         step("q2", [], 2)
@@ -183,6 +184,7 @@
     def others(marks):
         schedule(marks)
         handle_diag(0)
+        wo_copy().start()
         step("q1", [], 1)
         handle_diag(2)
         step("q2", [], 2)
@@ -195,27 +197,31 @@
     def _():
         others((9, 11, 13, 15, 17, 18))
 
-    def kv_part(part):
-        cols = slice(part * 2 * KB, (part + 1) * 2 * KB)
+    def kv_wait(part):
         with jax.named_scope(f"kvwait{part}"):
             arrived(X_C, 2 * part, 4)
-        with jax.named_scope(f"kv{part}"):
-            for i in range(2 * HC):
-                y = jnp.dot(xg[:, cols], wd[HC + i, cols], preferred_element_type=F32)
-                if part > 0:
-                    y = kvacc[i] + y
-                if part < 2:
-                    kvacc[i] = y
-                else:
-                    kv[i] = y.astype(BF16)
-
-    wo_copy().start()
-    kv_part(0)
+
+    def kv_heads(part, which):
+        cols = slice(part * 2 * KB, (part + 1) * 2 * KB)
+        for i in which:
+            y = jnp.dot(xg[:, cols], wd[HC + i, cols], preferred_element_type=F32)
+            if part > 0:
+                y = kvacc[i] + y
+            if part < 2:
+                kvacc[i] = y
+            else:
+                kv[i] = y.astype(BF16)
+
+    kv_wait(0)
+    with jax.named_scope("kv0"):
+        kv_heads(0, range(2 * HC))
     handle_diag(4)
-    kv_part(1)
-    kv_part(2)
-
-    def attend(part, n_keys):
+    kv_wait(1)
+    with jax.named_scope("kv1"):
+        kv_heads(1, range(2 * HC))
+    kv_wait(2)
+
+    def scores(part, n_keys):
         start = lo0 if part == 0 else hi0
         heads = range(HC)
         rows = start + lax.broadcasted_iota(jnp.int32, (64, n_keys), 0)
@@ -226,7 +232,11 @@
         m = [jnp.max(v, axis=-1, keepdims=True) for v in s]
         p = [jnp.exp(v - w) for v, w in zip(s, m)]
         l = [jnp.sum(v, axis=-1, keepdims=True) for v in p]
-        o = [jnp.dot(p[h].astype(BF16), kv[HC + h, :n_keys, :], preferred_element_type=F32) for h in heads]
+        return [v.astype(BF16) for v in p], l
+
+    def attend(part, n_keys, p, l):
+        heads = range(HC)
+        o = [jnp.dot(p[h], kv[HC + h, :n_keys, :], preferred_element_type=F32) for h in heads]
         for h in heads:
             z = (o[h] / l[h]).astype(BF16)
             oall[2 * part, h] = z[:32]
@@ -301,8 +311,14 @@
 
     def attend_both(order):
         for slot, part in enumerate(order):
+            n_keys = 128 if part == 0 else SEQ
             with jax.named_scope(f"attn{slot}"):
-                attend(part, 128 if part == 0 else SEQ)
+                if slot == 0:
+                    kv_heads(2, range(HC))
+                p, l = scores(part, n_keys)
+                if slot == 0:
+                    kv_heads(2, range(HC, 2 * HC))
+                attend(part, n_keys, p, l)
             o_send(part, slot)
 
     @pl.when(t == 1)

time: 27.7 us -> 27.7 us (level)
  no operation moved by 1% of the time
where the time goes in v7:
time: 27.7 us; the launch traced here: 27.5 us
  Pallas kernels  26.8 us (97%)
  local copies, waits for them, and re-layouts  0.68 us (2%)
    pallas_call x1, Pallas kernels, device_fn(): pl.pallas_call(kernel, out_shape=pltpu.VMEM((ROWS, D), BF16), in_specs=[a...  26.8 us
    unnamed x1, local copies, waits for them, and re-layouts  0.68 us

profile of v7, /device:TPU:0, one launch (start us, length us, event | category | flops | bytes accessed | tf_op | source)
XLA Modules:
  0.0 27.5 jit_solution(18057341904580523529)
XLA Ops:
  0.0 26.8 %mha.1 = bf16[32,3072]{1,0:T(8,128)(2,1)S(1)} custom-call(bf16[32,3072]{1,0:T(8,128)(2,1)} %x_hbm.1, bf16[6,2,256,2,2,4,128]{6,5,4,3,2,1,0:T(4,128)(2,1)} %bitcast.10, bf16[6,2,256,2,2,4,128]{6,5,4,3,2,1,0:T(4,128)(2,1)} %bitcast.11, bf16[6,2,256,2,2,4,128]{6,5,4,3,2,1,0:T(4,128)(2,1)} %bitcast.12, bf16[2048,3072]{1,0:T(8,128)(2,1)} %bitcast.13), custom_call_target="tpu_custom_call" | custom-call | tf_op jit(solution)/shard_map/mha/pallas_call | solution.py:400
  26.9 0.7 %copy.7 = bf16[32,3072]{1,0:T(8,128)(2,1)} copy(bf16[32,3072]{1,0:T(8,128)(2,1)S(1)} %mha.1) | data formatting | bytes 393216
